TPU v7x, 8 devices: a whole 2x2x1 slice. The times are simulated.
8 devices in a mesh: data: 2 (over z, y), graph: 4 (over x, core).
Axes of the slice: x: 2, y: 2, z: 1, core: 2. Of those that a mesh axis runs over, the one named last changes fastest.
Arguments:
- x_feat: bfloat16 [8192, 200], P(('data', 'graph')), parts along dimension 0
- dst_local: int32 [131072], P(('data', 'graph')), parts along dimension 0
- src_slot: int32 [131072], P(('data', 'graph')), parts along dimension 0
- edge_w: float32 [131072], P(('data', 'graph')), parts along dimension 0
- send_idx: int32 [2048], P(('data', 'graph')), parts along dimension 0
- hub_ids: int32 [32], P('data'), parts along dimension 0
- w_first: bfloat16 [200, 512], replicated
- b_first: float32 [512], replicated
- w_second: bfloat16 [512, 107], replicated
- grad_out: float32 [8192, 107], P(('data', 'graph')), parts along dimension 0
Outputs:
- output 1: float32 [8192, 200], P(('data', 'graph')), parts along dimension 0
- output 2: float32 [400, 512], P('data'), parts along dimension 0
- output 3: float32 [1024, 107], P('data'), parts along dimension 0
- output 4: float32 [1024], P('data'), parts along dimension 0
- output 5: float32 [214], P('data'), parts along dimension 0
There are 2 independent parts. A program takes and returns all parts, laid end to end along the dimension named above; an argument that names none is the same for every part.
All inputs are finite; a program needn't handle non-finite values.
Results may differ from a plain program's by a relative error of at most 0.001.
Values are sent between devices in bfloat16 or wider.
A program may use at most 1 GiB of HBM per device.

v0:
```python
import jax
import jax.numpy as jnp
from jax import lax
from jax.sharding import PartitionSpec as P

CONTRACT_ROWS = (((0,), (0,)), ((), ()))
CONTRACT_COLS = (((1,), (1,)), ((), ()))


def hub_collect(dev_rows, hub_owned, hub_row):
    picked = jnp.where(hub_owned[:, None], dev_rows[hub_row], jnp.zeros((), dev_rows.dtype))
    return lax.psum(picked, "graph")


def hub_return(dev_rows, hub_sum, hub_owned, hub_row):
    return dev_rows.at[hub_row].add(jnp.where(hub_owned[:, None], hub_sum, 0.0))


def propagate(features, graph_data, groups):
    send_loc, hub_owned, hub_row, dst_loc, src_loc, w_loc = graph_data
    num_nodes = features.shape[0]
    send_rows = send_loc.shape[0] // groups
    outgoing = features[send_loc].reshape(groups, send_rows, -1)
    halo_feat = lax.all_to_all(outgoing, "graph", 0, 0).reshape(groups * send_rows, -1)
    hub_feat = hub_collect(features, hub_owned, hub_row)
    feat_table = jnp.concatenate([features, halo_feat, hub_feat], axis=0)
    weighted = feat_table[src_loc].astype(jnp.float32) * w_loc[:, None]
    dev_sums = jax.ops.segment_sum(weighted, dst_loc, num_segments=num_nodes + hub_row.shape[0])
    hub_sum = lax.psum(dev_sums[num_nodes:], "graph")
    return hub_return(dev_sums[:num_nodes], hub_sum, hub_owned, hub_row)


def propagate_adjoint(grad_y, graph_data, groups):
    send_loc, hub_owned, hub_row, dst_loc, src_loc, w_loc = graph_data
    num_nodes = grad_y.shape[0]
    halo_rows = send_loc.shape[0]
    hub_grad = hub_collect(grad_y, hub_owned, hub_row)
    extended = jnp.concatenate([grad_y, hub_grad], axis=0)
    weighted = extended[dst_loc] * w_loc[:, None]
    table_grad = jax.ops.segment_sum(weighted, src_loc, num_segments=num_nodes + halo_rows + hub_row.shape[0])
    outgoing = table_grad[num_nodes:num_nodes + halo_rows].reshape(groups, halo_rows // groups, -1)
    returned = lax.all_to_all(outgoing, "graph", 0, 0).reshape(halo_rows, -1)
    grad_z = table_grad[:num_nodes].at[send_loc].add(returned)
    hub_back = lax.psum(table_grad[num_nodes + halo_rows:], "graph")
    return hub_return(grad_z, hub_back, hub_owned, hub_row)


def solution(mesh):
    groups = mesh.shape["graph"]
    vertex_spec = P(("data", "graph"))
    vertex_rows = P(("data", "graph"), None)
    part_spec = P("data")
    part_rows = P("data", None)
    replicated = P()

    def device_step(x_loc, dst_loc, src_loc, w_loc, send_loc, hub_ids, w_first, b_first, w_second, dy_out):
        num_nodes = x_loc.shape[0]
        my_index = lax.axis_index("graph")
        hub_owned = (hub_ids // num_nodes) == my_index
        hub_row = hub_ids % num_nodes
        graph_data = (send_loc, hub_owned, hub_row, dst_loc, src_loc, w_loc)
        z_first = jnp.dot(x_loc, w_first, preferred_element_type=jnp.float32).astype(jnp.bfloat16)
        pre_act = propagate(z_first, graph_data, groups) + b_first
        hidden = jax.nn.relu(pre_act).astype(jnp.bfloat16)
        grad_z2 = propagate_adjoint(dy_out, graph_data, groups).astype(jnp.bfloat16)
        grad_w2 = lax.psum(lax.dot_general(hidden, grad_z2, CONTRACT_ROWS, preferred_element_type=jnp.float32), "graph")
        grad_h = lax.dot_general(grad_z2, w_second, CONTRACT_COLS, preferred_element_type=jnp.float32)
        grad_pre = jnp.where(pre_act > 0, grad_h, 0.0)
        grad_b1 = lax.psum(grad_pre.sum(axis=0), "graph")
        grad_z1 = propagate_adjoint(grad_pre, graph_data, groups).astype(jnp.bfloat16)
        grad_w1 = lax.psum(lax.dot_general(x_loc, grad_z1, CONTRACT_ROWS, preferred_element_type=jnp.float32), "graph")
        grad_x = lax.dot_general(grad_z1, w_first, CONTRACT_COLS, preferred_element_type=jnp.float32)
        grad_b2 = lax.psum(dy_out.sum(axis=0), "graph")
        return grad_x, grad_w1, grad_w2, grad_b1, grad_b2

    return jax.shard_map(
        device_step,
        mesh=mesh,
        in_specs=(vertex_rows, vertex_spec, vertex_spec, vertex_spec, vertex_spec, part_spec, replicated, replicated, replicated, vertex_rows),
        out_specs=(vertex_rows, part_rows, part_rows, part_spec, part_spec),
        check_vma=False,
    )
```

profile of v0, /device:TPU:0, one launch (start us, length us, event | category | flops | bytes accessed | tf_op | source)
XLA Modules:
  0.0 1560.7 jit_solution(17959067852457614529)
XLA Ops:
  8.6 0.9 fusion.21
  9.5 1.2 copy.16
  11.4 8.9 psum.72
  20.3 158.2 %scatter_custom_fusion.2 = f32[1296,107]{1,0:T(8,128)S(1)} fusion(s32[16384]{0:T(1024)S(1)} %copy-done.10, f32[16384]{0:T(1024)S(1)} %copy-done.8, f32[]{:T(128)} %constant.20.clone.1, f32[1040,107]{1,0:T(8,128)S(1)} %pad_maximum_fusion.2, s32[16384]{0:T(1024)S(1)} %fusion.21), kind=kCustom, calls=%fused_computation.22 | custom fusion | flops 3506176 | bytes 1218244 | tf_op jit(solution)/shard_map/scatter-add | solution.py:40
  179.3 3.3 all-to-all-start.1
  183.8 1.9 gather_fusion
  185.7 1.3 all-to-all-done.1
  187.0 3.4 all-to-all-start
  190.5 11.7 psum.70
  202.1 2.3 scatter_fusion
  204.5 1.1 pad_maximum_fusion.1
  205.6 629.5 %scatter_custom_fusion = f32[1040,512]{1,0:T(8,128)} fusion(s32[16384]{0:T(1024)} %param.11, f32[16384]{0:T(1024)S(1)} %copy-done.8, f32[]{:T(128)} %constant.20.clone.1, bf16[1296,512]{1,0:T(8,128)(2,1)} %pad_maximum_fusion.1, s32[16384]{0:T(1024)S(1)} %fusion.20), kind=kCustom, calls=%fused_computation.17 | custom fusion | flops 25165824 | bytes 3588608 | tf_op jit(solution)/shard_map/scatter-add | solution.py:28
  835.2 1.9 slice_add_fusion
  837.1 10.7 all-reduce.1
  847.7 1.5 scatter_custom_fusion.1
  849.3 0.9 scatter_custom_fusion.4
  850.3 1.8 fusion.39
  852.1 2.2 gather_fusion.3
  854.3 10.5 psum.74
  864.8 3.1 pad_maximum_fusion
  867.9 625.5 %scatter_custom_fusion.5 = f32[1296,512]{1,0:T(8,128)S(1)} fusion(s32[16384]{0:T(1024)S(1)} %copy-done.10, f32[16384]{0:T(1024)S(1)} %copy-done.8, f32[]{:T(128)} %constant.20.clone.1, f32[1040,512]{1,0:T(8,128)} %pad_maximum_fusion, s32[16384]{0:T(1024)S(1)} %fusion.21), kind=kCustom, calls=%fused_computation.15 | custom fusion | flops 16777216 | bytes 4915204 | tf_op jit(solution)/shard_map/scatter-add | solution.py:40
  1493.5 0.8 slice.52
  1494.3 4.1 all-to-all-start.2
  1498.6 15.1 all-reduce
  1513.7 2.7 fusion.12
  1516.5 3.4 scatter_fusion.1
  1519.8 1.5 scatter_custom_fusion.7
  1521.4 1.1 convolution_bitcast_fusion
  1522.5 1.4 fusion.15
  1523.9 26.5 %all-reduce.5.cloned.1.call-done = (f32[200,512]{1,0:T(8,128)}, f32[512,107]{0,1:T(8,128)}) async-done(((f32[200,512]{1,0:T(8,128)}, f32[512,107]{0,1:T(8,128)}), (f32[200,512]{1,0:T(8,128)}, f32[512,107]{0,1:T(8,128)})) %all-reduce.5.cloned.1.call-update) | async-done | bytes 628752 | tf_op jit(solution)/shard_map/psum | solution.py:71
  1550.4 1.8 copy.24
  1552.2 1.6 copy.25
  (53 shorter events, 4.3 us)
Async XLA Ops:
  7.2 175.5 %copy-start = (bf16[1024,200]{0,1:T(8,128)(2,1)S(1)}, bf16[1024,200]{0,1:T(8,128)(2,1)}, u32[]{:S(2)}) copy-start(bf16[1024,200]{0,1:T(8,128)(2,1)} %param.10) | copy-start | bytes 1228804
  7.2 13.1 copy-start.8
  7.2 13.1 copy-start.10
  10.7 172.0 %copy-start.12 = (s32[256]{0:T(256)S(1)}, s32[256]{0:T(256)}, u32[]{:S(2)}) copy-start(s32[256]{0:T(256)} %param.14) | copy-start | bytes 3076
  10.7 172.0 %copy-start.6 = (bf16[200,512]{1,0:T(8,128)(2,1)S(1)}, bf16[200,512]{1,0:T(8,128)(2,1)}, u32[]{:S(2)}) copy-start(bf16[200,512]{1,0:T(8,128)(2,1)} %param.16) | copy-start | bytes 614404
  178.5 4.2 copy-start.4
  179.3 7.7 all-to-all-start.1
  187.0 17.5 %all-to-all-start = ((bf16[4,64,512]{2,1,0:T(8,128)(2,1)}), bf16[4,64,512]{2,1,0:T(8,128)(2,1)S(1)}, u32[]{:S(2)}, u32[]{:S(2)}) async-start(bf16[4,64,512]{2,1,0:T(8,128)(2,1)} %bitcast), calls=%async_computation | async-start | bytes 524288 | tf_op jit(solution)/shard_map/all_to_all | solution.py:24
  205.6 629.6 %copy-start.11 = (f32[512]{0:T(512)S(1)}, f32[512]{0:T(512)}, u32[]{:S(2)}) copy-start(f32[512]{0:T(512)} %param.17) | copy-start | bytes 6148
  835.2 1.9 slice-start.1
  835.2 1.9 slice-start.2
  837.1 13.2 copy-start.9
  849.3 2.8 copy-start.2
  850.2 1.8 copy-start.3
  1493.4 5.2 copy-start.1
  1493.4 5.0 copy-start.5
  1494.3 22.2 %all-to-all-start.2 = ((f32[4,64,512]{2,1,0:T(8,128)}), f32[4,64,512]{2,1,0:T(8,128)}, u32[]{:S(2)}, u32[]{:S(2)}) async-start(f32[4,64,512]{2,1,0:T(8,128)} %bitcast.13), calls=%async_computation.2 | async-start | bytes 1048576 | tf_op jit(solution)/shard_map/all_to_all | solution.py:42
  1498.4 52.0 %all-reduce.5.cloned.1.call-start = ((), (), s32[]{:S(2)}) async-start(), calls=%async_computation.3 | async-start | bytes 1277952 | tf_op jit(solution)/shard_map/psum | solution.py:71
  1498.6 17.8 %slice-start = ((f32[1296,512]{1,0:T(8,128)}), f32[1024,512]{1,0:T(8,128)S(1)}, s32[]{:S(2)}) async-start(f32[1296,512]{1,0:T(8,128)} %copy-done.1), calls=%async_computation.4 | async-start | bytes 4194304 | tf_op jit(solution)/shard_map/slice | solution.py:43
  1521.4 1.2 copy-start.7
Sparse Core Ops, SparseCore 0:
  1423.5 128.1 all-reduce.4
where the time goes:
time: 1570 us; the launch traced here: 1560 us
  other arithmetic  592 us (38%)
  blocking collectives  421 us (27%)
  starting transfers between devices  387 us (25%)
  waiting for transfers between devices  129 us (8%)
    all_to_all x2, starting transfers between devices, propagate_adjoint(): returned = lax.all_to_all(outgoing, 'graph', 0, 0).reshape(halo_rows, -1)  384 us
    psum x1, blocking collectives, propagate(): hub_sum = lax.psum(dev_sums[num_nodes:], 'graph')  375 us
    scatter-add x2, other arithmetic, propagate_adjoint(): jax.ops.segment_sum(weighted, src_loc, num_segments=num_nodes + halo_rows...  354 us
    scatter-add x1, other arithmetic, propagate(): jax.ops.segment_sum(weighted, dst_loc, num_segments=num_nodes + hub_row.s...  219 us
    psum x1, waiting for transfers between devices, device_step(): lax.psum(lax.dot_general(x_loc, grad_z1, CONTRACT_ROWS, preferred_element...  127 us
  transfers between devices with their start and end apart: 4, of which 2 were waited for; matrix products, arithmetic and copies ran while one was open for 1% of the time, Pallas kernels for 0%

commit v1 on v0

v1 whole, which is shorter than its diff:
```python
import functools

import jax
import jax.numpy as jnp
from jax import lax
from jax.experimental import pallas as pl
from jax.experimental.pallas import tpu as pltpu
from jax.sharding import PartitionSpec as P

F32, BF16 = jnp.float32, jnp.bfloat16
NODES, SEND, HALO, HUBS = 1024, 64, 256, 16
TABLE = NODES + HALO + HUBS
TILES = 9
COLS = TILES * 128
ROWS = TILES * TABLE
EDGES = 16384
HID, OUT, FIN = 512, 107, 200
ACCS = 4
UNROLL = 4
NT = (((1,), (1,)), ((), ()))


def split3(x):
    hi = x.astype(BF16)
    rest = x - hi.astype(F32)
    mid = rest.astype(BF16)
    return hi, mid, (rest - mid.astype(F32)).astype(BF16)


def dot(a, b):
    return jnp.dot(a, b, preferred_element_type=F32)


def dot_nt(a, b):
    return lax.dot_general(a, b, NT, preferred_element_type=F32)


def build_kernel(hub_ref, dst_ref, src_ref, w_ref, hi_ref, mid_ref, lo_ref, val_ref, row_ref, lane_ref, row_smem, sem, *accs):
    base = lax.axis_index("graph") * NODES
    dst, src = dst_ref[...], src_ref[...]
    new_dst, new_src = dst, src
    for k in range(HUBS):
        local = hub_ref[k] - base
        local = jnp.where((local >= 0) & (local < NODES), local, -1)
        new_dst = jnp.where(dst == local, NODES + k, new_dst)
        new_src = jnp.where(src == local, NODES + HALO + k, new_src)
    row_ref[...] = (new_dst >> 7) * TABLE + new_src
    lane_ref[...] = new_dst & 127
    copy = pltpu.make_async_copy(row_ref, row_smem, sem)
    copy.start()

    def zero(i, carry):
        for acc in accs:
            acc[pl.ds(pl.multiple_of(i * 48, 8), 48), :] = jnp.zeros((48, 128), F32)
        return carry

    lax.fori_loop(0, ROWS // 48, zero, 0)
    iota = lax.broadcasted_iota(jnp.int32, (8, 128), 1)

    def prep(g, carry):
        at = pl.multiple_of(g * 8, 8)
        lanes, weights = lane_ref[pl.ds(at, 8), :], w_ref[pl.ds(at, 8), :]
        for c in range(128):
            hit = jnp.broadcast_to(lanes[:, c:c + 1], (8, 128)) == iota
            val = jnp.where(hit, jnp.broadcast_to(weights[:, c:c + 1], (8, 128)), 0.0)
            val_ref[pl.ds(pl.multiple_of(g * 1024 + c * 8, 8), 8), :] = val
        return carry

    lax.fori_loop(0, 16, prep, 0)
    copy.wait()

    def scatter(t, carry):
        per_group = 128 // UNROLL
        group = t // per_group
        col = (t - group * per_group) * UNROLL
        vbase = pl.multiple_of(t * UNROLL * 8, 8 * UNROLL)
        n = 0
        for c in range(UNROLL):
            for s in range(8):
                acc = accs[n % ACCS]
                n += 1
                r = row_smem[group * 8 + s, col + c]
                acc[pl.ds(r, 1), :] = acc[pl.ds(r, 1), :] + val_ref[pl.ds(vbase + c * 8 + s, 1), :]
        return carry

    lax.fori_loop(0, EDGES // (8 * UNROLL), scatter, 0)

    def finish(i, carry):
        at = pl.multiple_of(i * 48, 16)
        for t in range(TILES):
            part = pl.ds(pl.multiple_of(t * TABLE + i * 48, 8), 48)
            total = accs[0][part, :]
            for acc in accs[1:]:
                total = total + acc[part, :]
            for piece, ref in zip(split3(total), (hi_ref, mid_ref, lo_ref)):
                ref[pl.ds(at, 48), t * 128:(t + 1) * 128] = piece
        return carry

    lax.fori_loop(0, TABLE // 48, finish, 0)


def build(hub_ids, dst, src, w):
    piece = jax.ShapeDtypeStruct((TABLE, COLS), BF16)
    square = lambda a: a.reshape(128, 128)
    vmem = pl.BlockSpec(memory_space=pltpu.VMEM)
    return pl.pallas_call(
        build_kernel,
        out_shape=(piece,) * 3,
        in_specs=[pl.BlockSpec(memory_space=pltpu.SMEM)] + [vmem] * 3,
        out_specs=(vmem,) * 3,
        scratch_shapes=[
            pltpu.VMEM((EDGES, 128), F32),
            pltpu.VMEM((128, 128), jnp.int32),
            pltpu.VMEM((128, 128), jnp.int32),
            pltpu.SMEM((128, 128), jnp.int32),
            pltpu.SemaphoreType.DMA,
        ] + [pltpu.VMEM((ROWS, 128), F32)] * ACCS,
        compiler_params=pltpu.CompilerParams(vmem_limit_bytes=48 << 20),
        name="build",
    )(hub_ids, square(dst), square(src), square(w))


def step_kernel(
    hi_ref, mid_ref, lo_ref, x_ref, w1_ref, b1_ref, w2_ref, dh_ref, send_ref, hub_ref,
    dx_ref, dw1_ref, dw2_ref, db1_ref, db2_ref,
    row_s, pt_s, xs, xr, hs, hr, z_s, yt_s, d2_s, g2_s, g2h_s, rb, sb, ys, yr, dy_s, g1_s, sd, rd, ret_s, dz1_s,
    xt_s, a2, half2, got2, tot2, a1, half1, got1, tot1, send_sem, recv_sem,
):
    me = lax.axis_index("graph")
    sibling = me + 1 - 2 * lax.rem(me, 2)
    across = lax.rem(me + 2, 4)
    core = lax.rem(me, 2)
    mesh_id = pl.DeviceIdType.MESH
    peers = [lax.rem(me + d, 4) for d in (1, 2, 3)]
    barrier = pltpu.get_barrier_semaphore()
    for q in peers:
        pl.semaphore_signal(barrier, inc=1, device_id={"graph": q}, device_id_type=mesh_id)
    pl.semaphore_wait(barrier, 3)
    used = [0]

    def remote(src, dst, q):
        i = used[0]
        used[0] += 1
        copy = pltpu.make_async_remote_copy(
            src_ref=src, dst_ref=dst, send_sem=send_sem.at[i], recv_sem=recv_sem.at[i],
            device_id={"graph": q}, device_id_type=mesh_id)
        copy.start()
        return copy

    pieces = (hi_ref, mid_ref, lo_ref)
    row_s[...] = jnp.full((1, 384), -1.0, F32)
    row_s[:, :HALO] = send_ref[...].astype(F32)
    hub_local = hub_ref[...] - me * NODES
    row_s[:, HALO:HALO + HUBS] = jnp.where((hub_local >= 0) & (hub_local < NODES), hub_local, -1).astype(F32)
    row = row_s[...]
    column = jnp.transpose(jnp.broadcast_to(row, (128, 384)))
    lane = lax.broadcasted_iota(jnp.int32, (272, 128), 1).astype(F32)
    picks = jnp.concatenate(
        [jnp.where(column[:272] == lane + float(j * 128), 1.0, 0.0).astype(BF16) for j in range(8)], axis=1)
    sub = lax.broadcasted_iota(jnp.int32, (NODES, 384), 0).astype(F32)
    pt_s[...] = jnp.where(sub == row, 1.0, 0.0).astype(BF16)
    x = x_ref[...]
    sent = dot(picks, x).astype(BF16)
    hub_col = column[HALO:HALO + HUBS]
    alias = [jnp.where((hub_col == row[:, j * 128:(j + 1) * 128]) & (hub_col >= 0.0), 1.0, 0.0) for j in range(2)]
    for q in range(4):
        xs[q, :SEND, :] = sent[q * SEND:(q + 1) * SEND]
        xs[q, SEND:SEND + HUBS, :] = sent[HALO:]
        part = alias[q // 2][:, (q % 2) * SEND:(q % 2 + 1) * SEND]
        xs[q, SEND + HUBS:, :SEND] = part.astype(BF16)
        xs[q, SEND + HUBS:, SEND:] = jnp.zeros((HUBS, FIN - SEND), BF16)
    d2_s[...] = jnp.zeros((COLS, 384), BF16)
    dh = dh_ref[...]
    for j, piece in enumerate(split3(dh)):
        d2_s[:NODES, j * 128:j * 128 + OUT] = piece
    hub_pick = picks[HALO:]
    hub_dh = dot(hub_pick, d2_s[:NODES, :])
    hs[...] = (hub_dh[:, :128] + hub_dh[:, 128:256]) + hub_dh[:, 256:]
    xr[me] = jnp.zeros((96, FIN), BF16)
    hr[me] = hs[...]
    round_a = []
    for q in peers:
        round_a.append(remote(xs.at[q], xr.at[me], q))
        round_a.append(remote(hs, hr.at[me], q))
    db2_ref[...] = jnp.sum(dh, axis=0, keepdims=True)

    def reduce_group(own, half, got, total):
        remote(own.at[1 - core], got.at[0], sibling).wait()
        half[...] = own[core] + got[0]
        remote(half, got.at[1], across).wait()
        total[core] = half[...] + got[1]
        remote(total.at[core], total.at[core], sibling).wait()

    xt_s[:FIN, :] = jnp.transpose(jnp.concatenate([x, jnp.zeros((NODES, 56), BF16)], axis=1).astype(F32))[:FIN].astype(BF16)
    w1t = jnp.transpose(jnp.concatenate([w1_ref[...], jnp.zeros((56, HID), BF16)], axis=0).astype(F32)).astype(BF16)[:, :FIN]
    z_s[:, :NODES] = dot_nt(w1t, x).astype(BF16)

    def forward_own(at):
        z = z_s[:, :NODES]
        acc = dot(z, hi_ref[:NODES, at])
        acc = acc + dot(z, mid_ref[:NODES, at])
        yt_s[:, at] = acc + dot(z, lo_ref[:NODES, at])

    def over_columns(body):
        def turn(n, carry):
            body(pl.ds(pl.multiple_of(n * 256, 256), 256))
            return carry

        lax.fori_loop(0, 4, turn, 0)

    over_columns(forward_own)
    forward_own(pl.ds(NODES, 128))

    def wait_all(copies):
        for copy in copies:
            copy.wait()

    wait_all(round_a)
    halo_x = jnp.concatenate([xr[q, :SEND, :] for q in range(4)], axis=0)
    own_hub_x = sent[HALO:].astype(F32)
    hub_x = own_hub_x
    for q in range(4):
        hub_x = hub_x + xr[q, SEND:SEND + HUBS, :].astype(F32)
    z_s[:, NODES:NODES + HALO] = dot_nt(w1t, halo_x).astype(BF16)
    z_hub = dot_nt(w1t, hub_x.astype(BF16)).astype(BF16)

    def forward_far(at):
        z = z_s[:, NODES:NODES + HALO]
        acc = yt_s[:, at]
        for ref in pieces:
            acc = acc + dot(z, ref[NODES:NODES + HALO, at])
        for ref in pieces:
            acc = acc + dot(z_hub, ref[NODES + HALO:, at])
        yt_s[:, at] = acc

    forward_far(pl.ds(NODES, 128))
    ys[...] = jnp.transpose(yt_s[:, NODES:])[:HUBS]
    yr[me] = ys[...]
    round_y = [remote(ys, yr.at[me], q) for q in peers]
    over_columns(forward_far)

    hub_dh = (hr[0] + hr[1]) + (hr[2] + hr[3])
    for j, piece in enumerate(split3(hub_dh)):
        d2_s[NODES:NODES + HUBS, j * 128:(j + 1) * 128] = piece

    def grad2(rows):
        a = dot(hi_ref[rows, :], d2_s[:, :256])
        b = dot(mid_ref[rows, :], d2_s[:, :256])
        c = dot(hi_ref[rows, :], d2_s[:, 256:]) + dot(lo_ref[rows, :], d2_s[:, :128])
        return ((c + b[:, 128:]) + (a[:, 128:] + b[:, :128])) + a[:, :128]

    g2h_s[...] = grad2(pl.ds(NODES, HALO + HUBS))
    far = g2h_s[:HALO, :]
    alias_row = jnp.concatenate([xr[q, SEND + HUBS:, :SEND] for q in range(4)], axis=1)
    hub_g2 = g2h_s[HALO:, :]
    for piece in split3(far):
        hub_g2 = hub_g2 + dot(alias_row, piece)
    for q in range(4):
        sb[q, :SEND, :] = far[q * SEND:(q + 1) * SEND]
        sb[q, SEND:, :] = hub_g2
    rb[me] = sb[me]
    round_b = [remote(sb.at[q], rb.at[me], q) for q in peers]

    def grad2_own(m, carry):
        at = pl.ds(pl.multiple_of(m * 256, 256), 256)
        g2_s[at, :] = grad2(at)
        return carry

    lax.fori_loop(0, 4, grad2_own, 0)
    wait_all(round_y)
    wait_all(round_b)

    hub_full = (rb[0, SEND:, :] + rb[1, SEND:, :]) + (rb[2, SEND:, :] + rb[3, SEND:, :])
    hub_dz2 = hub_full.astype(BF16)
    keep = lax.broadcasted_iota(jnp.int32, (4, SEND, 128), 0) != me
    back = jnp.where(keep, rb[:, :SEND, :], 0.0).reshape(HALO, 128)
    own = g2_s[...]
    halo_pick = pt_s[:, :HALO]
    hub_put = pt_s[:, HALO:HALO + HUBS]
    for piece in split3(back):
        own = own + dot(halo_pick, piece)
    is_hub = dot(hub_put, jnp.ones((HUBS, 128), BF16)) > 0.5
    dz2 = jnp.where(is_hub, dot(hub_put, hub_dz2), own).astype(BF16)

    y_hub = (yr[0] + yr[1]) + (yr[2] + yr[3])
    b1 = b1_ref[...]
    b1_col = jnp.transpose(jnp.broadcast_to(b1, (128, HID)))
    hub_sel = picks[HALO:]
    for piece in split3(jnp.transpose(jnp.concatenate([y_hub, jnp.zeros((112, HID), F32)], axis=0))):
        yt_s[:, :NODES] += dot(piece[:, :HUBS], hub_sel)
    pre = yt_s[:, :NODES] + jnp.concatenate([b1_col] * 8, axis=1)
    hidden_t = jnp.maximum(pre, 0.0).astype(BF16)
    live = jnp.transpose(jnp.where(pre > 0.0, 1.0, 0.0))
    dw2 = dot(hidden_t, dz2)
    db2 = jnp.concatenate([db2_ref[...], jnp.zeros((1, 128 - OUT), F32)], axis=1)
    for h in range(2):
        a2[h, :256, :] = dw2[h * 256:(h + 1) * 256]
        a2[h, 256:, :] = jnp.broadcast_to(db2, (8, 128))
    reduce_group(a2, half2, got2, tot2)
    w2 = w2_ref[...]
    grad_h = dot_nt(dz2[:, :OUT], w2)
    dy = jnp.where(live > 0.5, grad_h, 0.0)
    hub_dy = jnp.where(y_hub + b1 > 0.0, dot_nt(hub_dz2[:, :OUT], w2), 0.0)
    db1 = jnp.sum(dy, axis=0, keepdims=True)
    for j, piece in enumerate(split3(dy)):
        dy_s[j, :NODES, :] = piece
    for j, piece in enumerate(split3(hub_dy)):
        dy_s[j, NODES:NODES + HUBS, :] = piece
        dy_s[j, NODES + HUBS:, :] = jnp.zeros((112, HID), BF16)

    def grad1(rows):
        acc = dot(lo_ref[rows, :], dy_s[0])
        acc = acc + dot(mid_ref[rows, :], dy_s[1])
        acc = acc + dot(hi_ref[rows, :], dy_s[2])
        acc = acc + dot(mid_ref[rows, :], dy_s[0])
        acc = acc + dot(hi_ref[rows, :], dy_s[1])
        return acc + dot(hi_ref[rows, :], dy_s[0])

    ret_s[...] = grad1(pl.ds(NODES, HALO + HUBS))
    for q in range(4):
        sd[q, :SEND, :] = ret_s[q * SEND:(q + 1) * SEND, :]
        sd[q, SEND:, :] = ret_s[HALO:, :]
    rd[me] = sd[me]
    round_d = [remote(sd.at[q], rd.at[me], q) for q in peers]

    for m in range(2):
        g1_s[m * 512:(m + 1) * 512, :] = grad1(pl.ds(m * 512, 512))
    wait_all(round_d)
    back = jnp.where(lax.broadcasted_iota(jnp.int32, (4, SEND, HID), 0) != me, rd[:, :SEND, :], 0.0).reshape(HALO, HID)
    hub_back = (rd[0, SEND:, :] + rd[1, SEND:, :]) + (rd[2, SEND:, :] + rd[3, SEND:, :])
    dz1 = g1_s[...]
    for piece in split3(back):
        dz1 = dz1 + dot(halo_pick, piece)
    for piece in split3(hub_back):
        dz1 = dz1 + dot(hub_put, piece)
    dz1_s[...] = dz1.astype(BF16)
    dw1 = dot(xt_s[:FIN, :], dz1_s[...])

    dx_ref[...] = dot_nt(dz1_s[...], w1_ref[...])
    for h in range(2):
        a1[h, :FIN, :] = dw1[:, h * 256:(h + 1) * 256]
        a1[h, FIN:, :] = jnp.broadcast_to(db1[:, h * 256:(h + 1) * 256], (8, 256))
    reduce_group(a1, half1, got1, tot1)
    for h in range(2):
        dw1_ref[:, h * 256:(h + 1) * 256] = tot1[h, :FIN, :]
        db1_ref[:, h * 256:(h + 1) * 256] = tot1[h, FIN:FIN + 1, :]
    for h in range(2):
        dw2_ref[h * 256:(h + 1) * 256, :] = tot2[h, :256, :OUT]
    db2_ref[...] = tot2[0, 256:257, :OUT]


def step(hi, mid, lo, x, w1, b1, w2, dh, send, hubs):
    vmem = pl.BlockSpec(memory_space=pltpu.VMEM)
    out = lambda *shape: jax.ShapeDtypeStruct(shape, F32)
    f32 = lambda *shape: pltpu.VMEM(shape, F32)
    b16 = lambda *shape: pltpu.VMEM(shape, BF16)
    return pl.pallas_call(
        step_kernel,
        out_shape=(out(NODES, FIN), out(FIN, HID), out(HID, OUT), out(1, HID), out(1, OUT)),
        in_specs=[vmem] * 10,
        out_specs=(vmem,) * 5,
        scratch_shapes=[
            f32(1, 384), b16(NODES, 384), b16(4, 96, FIN), b16(4, 96, FIN), f32(HUBS, 128), f32(4, HUBS, 128),
            b16(HID, NODES + HALO), f32(HID, COLS), b16(COLS, 384), f32(NODES, 128), f32(HALO + HUBS, 128),
            f32(4, SEND + HUBS, 128), f32(4, SEND + HUBS, 128), f32(HUBS, HID), f32(4, HUBS, HID),
            b16(3, COLS, HID), f32(NODES, HID), f32(4, SEND + HUBS, HID), f32(4, SEND + HUBS, HID),
            f32(HALO + HUBS, HID), b16(NODES, HID), b16(FIN + 8, NODES),
            f32(2, 264, 128), f32(264, 128), f32(2, 264, 128), f32(2, 264, 128),
            f32(2, 208, 256), f32(208, 256), f32(2, 208, 256), f32(2, 208, 256),
            pltpu.SemaphoreType.DMA((24,)), pltpu.SemaphoreType.DMA((24,)),
        ],
        compiler_params=pltpu.CompilerParams(collective_id=0, has_side_effects=True, vmem_limit_bytes=48 << 20),
        name="step",
    )(hi, mid, lo, x, w1, b1, w2, dh, send, hubs)


def solution(mesh):
    vertex_spec = P(("data", "graph"))
    vertex_rows = P(("data", "graph"), None)
    part_spec = P("data")
    part_rows = P("data", None)
    replicated = P()

    def device_step(x, dst, src, w, send, hub_ids, w_first, b_first, w_second, dy_out):
        hi, mid, lo = build(hub_ids, dst, src, w)
        dx, dw1, dw2, db1, db2 = step(
            hi, mid, lo, x, w_first, b_first.reshape(1, HID), w_second, dy_out, send.reshape(1, HALO), hub_ids.reshape(1, HUBS))
        return dx, dw1, dw2, db1.reshape(HID), db2.reshape(OUT)

    return jax.shard_map(
        device_step,
        mesh=mesh,
        in_specs=(vertex_rows, vertex_spec, vertex_spec, vertex_spec, vertex_spec, part_spec, replicated, replicated, replicated, vertex_rows),
        out_specs=(vertex_rows, part_rows, part_rows, part_spec, part_spec),
        check_vma=False,
    )
```

time: 1570 us -> 114 us (0.07)
  other arithmetic: 592 us -> 0 us
  blocking collectives: 421 us -> 0 us
  starting transfers between devices: 387 us -> 0 us
  waiting for transfers between devices: 129 us -> 0 us
  Pallas kernels: 0 us -> 98.5 us
    scatter-add x8 -> x0, other arithmetic: 583 us -> none  [the longest x2 354 us: propagate_adjoint(): jax.ops.segment_sum(weighted, src_loc, num_segments=num_nodes + halo_rows...]
    psum x5 -> x0, blocking collectives: 421 us -> none  [the longest x1 375 us: propagate(): hub_sum = lax.psum(dev_sums[num_nodes:], 'graph')]
    all_to_all x3 -> x0, starting transfers between devices: 387 us -> none  [the longest x2 384 us: propagate_adjoint(): returned = lax.all_to_all(outgoing, 'graph', 0, 0).reshape(halo_rows, -1)]
    psum x1 -> x0, waiting for transfers between devices: 127 us -> none  [device_step(): lax.psum(lax.dot_general(x_loc, grad_z1, CONTRACT_ROWS, preferred_element...]
    pallas_call x0 -> x2, Pallas kernels: none -> 98.5 us  [the longest x1 52.8 us: step(): pl.pallas_call(step_kernel, out_shape=(out(NODES, FIN), out(FIN, HID), ou...]
  transfers between devices with their start and end apart: 4 -> 0, of which waited for: 2 -> 0; matrix products, arithmetic and copies ran while one was open for 1% -> 0% of each run, Pallas kernels for 0% -> 0%
where the time goes in v1:
time: 114 us
  Pallas kernels  98.5 us (86%)
  local copies, waits for them, and re-layouts  14.4 us (13%)
    pallas_call x1, Pallas kernels, step(): pl.pallas_call(step_kernel, out_shape=(out(NODES, FIN), out(FIN, HID), ou...  52.8 us
    pallas_call x1, Pallas kernels, build(): pl.pallas_call(build_kernel, out_shape=(piece,) * 3, in_specs=[pl.BlockSp...  45.7 us
    unnamed x24, local copies, waits for them, and re-layouts  14.4 us

profile of v1, /device:TPU:0, one launch (start us, length us, event | category | flops | bytes accessed | tf_op | source)
XLA Modules:
  0.0 113.6 jit_solution(7247194751705946341)
XLA Ops:
  0.6 1.0 copy.16.w2_ref
  1.7 1.2 %copy.15.x_ref = bf16[1024,200]{1,0:T(8,128)(2,1)S(1)} copy(bf16[1024,200]{0,1:T(8,128)(2,1)} %param.10) | data formatting | bytes 819200 | tf_op args[0]
  2.9 1.2 %copy.17.dh_ref = f32[1024,107]{1,0:T(8,128)S(1)} copy(f32[1024,107]{0,1:T(8,128)} %param.19) | data formatting | bytes 876544 | tf_op args[9]
  4.1 0.0 copy-start.2
  4.1 0.8 copy-done.2
  4.9 0.0 copy-start.3
  4.9 0.8 copy-done.3
  5.8 0.0 copy-start.4
  5.8 0.8 copy-done.4
  6.6 0.0 copy-start.5
  6.6 0.7 copy-done.5
  7.3 45.7 %build.1 = (bf16[1296,1152]{1,0:T(8,128)(2,1)S(1)}, bf16[1296,1152]{1,0:T(8,128)(2,1)S(1)}, bf16[1296,1152]{1,0:T(8,128)(2,1)}) custom-call(s32[16]{0:T(128)S(1)} %copy-done.5, s32[128,128]{1,0:T(8,128)S(1)} %bitcast.8, s32[128,128]{1,0:T(8,128)S(1)} %bitcast.9, f32[128,128]{1,0:T(8,128)S(1)} %bitcast.10), custom_call_target="tpu_custom_call" | custom-call | tf_op jit(solution)/shard_map/build/pallas_call | solution.py:106
  53.0 0.0 copy-start
  53.0 1.6 %copy-done = bf16[1296,1152]{1,0:T(8,128)(2,1)} copy-done((bf16[1296,1152]{1,0:T(8,128)(2,1)}, bf16[1296,1152]{1,0:T(8,128)(2,1)S(1)}, u32[]{:S(2)}) %copy-start) | copy-done | bytes 2986008
  54.7 0.0 copy-start.1
  54.7 0.9 copy-done.1
  55.6 0.0 copy-start.6
  55.6 0.7 copy-done.6
  56.3 0.0 copy-start.7
  56.3 0.7 copy-done.7
  57.0 52.8 %step.1 = (f32[1024,200]{1,0:T(8,128)S(1)}, f32[200,512]{1,0:T(8,128)S(1)}, f32[512,107]{1,0:T(8,128)S(1)}, f32[1,512]{1,0:T(1,128)S(1)}, f32[1,107]{1,0:T(1,128)S(1)}) custom-call(bf16[1296,1152]{1,0:T(8,128)(2,1)S(1)} %get-tuple-element.13.hi_ref, bf16[1296,1152]{1,0:T(8,128)(2,1)} %copy-done, bf16[1296,1152]{1,0:T(8,128)(2,1)} %get-tuple-element.15.lo_ref, ...), custom_call_target="tpu_custom_call" | custom-call | tf_op jit(solution)/shard_map/step/pallas_call | solution.py:357
  109.7 1.2 %copy.18 = f32[1024,200]{0,1:T(8,128)} copy(f32[1024,200]{1,0:T(8,128)S(1)} %get-tuple-element.21) | data formatting | bytes 1638400
  111.0 0.8 copy.19
  111.8 0.8 copy.23
  112.5 0.6 copy.24
  113.1 0.5 copy.25
Async XLA Ops:
  4.1 0.8 copy-start.2
  4.9 0.8 copy-start.3
  5.8 0.8 copy-start.4
  6.6 0.7 copy-start.5
  53.0 1.6 %copy-start = (bf16[1296,1152]{1,0:T(8,128)(2,1)}, bf16[1296,1152]{1,0:T(8,128)(2,1)S(1)}, u32[]{:S(2)}) copy-start(bf16[1296,1152]{1,0:T(8,128)(2,1)S(1)} %get-tuple-element.14.mid_ref) | copy-start | bytes 8957956
  54.7 0.9 copy-start.1
  55.6 0.7 copy-start.6
  56.3 0.7 copy-start.7

commit v2 on v1

--- a/solution.py
+++ b/solution.py
@@ -121,10 +121,10 @@
 
 
 def step_kernel(
-    hi_ref, mid_ref, lo_ref, x_ref, w1_ref, b1_ref, w2_ref, dh_ref, send_ref, hub_ref,
-    dx_ref, dw1_ref, dw2_ref, db1_ref, db2_ref,
+    hi_ref, mid_ref, lo_ref, xt_ref, w1_ref, b1_ref, w2t_ref, dht_ref, send_ref, hub_ref,
+    dxt_ref, dw1_ref, dw2t_ref, db1_ref, db2_ref,
     row_s, pt_s, xs, xr, hs, hr, z_s, yt_s, d2_s, g2_s, g2h_s, rb, sb, ys, yr, dy_s, g1_s, sd, rd, ret_s, dz1_s,
-    xt_s, a2, half2, got2, tot2, a1, half1, got1, tot1, send_sem, recv_sem,
+    a2, half2, got2, tot2, a1, half1, got1, tot1, send_sem, recv_sem,
 ):
     me = lax.axis_index("graph")
     sibling = me + 1 - 2 * lax.rem(me, 2)
@@ -159,8 +159,8 @@
         [jnp.where(column[:272] == lane + float(j * 128), 1.0, 0.0).astype(BF16) for j in range(8)], axis=1)
     sub = lax.broadcasted_iota(jnp.int32, (NODES, 384), 0).astype(F32)
     pt_s[...] = jnp.where(sub == row, 1.0, 0.0).astype(BF16)
-    x = x_ref[...]
-    sent = dot(picks, x).astype(BF16)
+    xt = xt_ref[...]
+    sent = dot_nt(picks, xt).astype(BF16)
     hub_col = column[HALO:HALO + HUBS]
     alias = [jnp.where((hub_col == row[:, j * 128:(j + 1) * 128]) & (hub_col >= 0.0), 1.0, 0.0) for j in range(2)]
     for q in range(4):
@@ -170,9 +170,10 @@
         xs[q, SEND + HUBS:, :SEND] = part.astype(BF16)
         xs[q, SEND + HUBS:, SEND:] = jnp.zeros((HUBS, FIN - SEND), BF16)
     d2_s[...] = jnp.zeros((COLS, 384), BF16)
-    dh = dh_ref[...]
+    dht = dht_ref[...]
+    dh = jnp.transpose(jnp.concatenate([dht, jnp.zeros((128 - OUT, NODES), F32)], axis=0))
     for j, piece in enumerate(split3(dh)):
-        d2_s[:NODES, j * 128:j * 128 + OUT] = piece
+        d2_s[:NODES, j * 128:(j + 1) * 128] = piece
     hub_pick = picks[HALO:]
     hub_dh = dot(hub_pick, d2_s[:NODES, :])
     hs[...] = (hub_dh[:, :128] + hub_dh[:, 128:256]) + hub_dh[:, 256:]
@@ -182,7 +183,7 @@
     for q in peers:
         round_a.append(remote(xs.at[q], xr.at[me], q))
         round_a.append(remote(hs, hr.at[me], q))
-    db2_ref[...] = jnp.sum(dh, axis=0, keepdims=True)
+    db2 = jnp.sum(dh, axis=0, keepdims=True)
 
     def reduce_group(own, half, got, total):
         remote(own.at[1 - core], got.at[0], sibling).wait()
@@ -191,9 +192,8 @@
         total[core] = half[...] + got[1]
         remote(total.at[core], total.at[core], sibling).wait()
 
-    xt_s[:FIN, :] = jnp.transpose(jnp.concatenate([x, jnp.zeros((NODES, 56), BF16)], axis=1).astype(F32))[:FIN].astype(BF16)
     w1t = jnp.transpose(jnp.concatenate([w1_ref[...], jnp.zeros((56, HID), BF16)], axis=0).astype(F32)).astype(BF16)[:, :FIN]
-    z_s[:, :NODES] = dot_nt(w1t, x).astype(BF16)
+    z_s[:, :NODES] = dot(w1t, xt).astype(BF16)
 
     def forward_own(at):
         z = z_s[:, :NODES]
@@ -291,16 +291,16 @@
     pre = yt_s[:, :NODES] + jnp.concatenate([b1_col] * 8, axis=1)
     hidden_t = jnp.maximum(pre, 0.0).astype(BF16)
     live = jnp.transpose(jnp.where(pre > 0.0, 1.0, 0.0))
-    dw2 = dot(hidden_t, dz2)
-    db2 = jnp.concatenate([db2_ref[...], jnp.zeros((1, 128 - OUT), F32)], axis=1)
+    dw2t = jnp.transpose(dot(hidden_t, dz2))
     for h in range(2):
-        a2[h, :256, :] = dw2[h * 256:(h + 1) * 256]
-        a2[h, 256:, :] = jnp.broadcast_to(db2, (8, 128))
+        a2[h, :112, :] = dw2t[:112, h * 256:(h + 1) * 256]
+        a2[h, 112:, :128] = jnp.broadcast_to(db2, (8, 128))
+        a2[h, 112:, 128:] = jnp.zeros((8, 128), F32)
     reduce_group(a2, half2, got2, tot2)
-    w2 = w2_ref[...]
-    grad_h = dot_nt(dz2[:, :OUT], w2)
+    w2t = w2t_ref[...]
+    grad_h = dot(dz2[:, :OUT], w2t)
     dy = jnp.where(live > 0.5, grad_h, 0.0)
-    hub_dy = jnp.where(y_hub + b1 > 0.0, dot_nt(hub_dz2[:, :OUT], w2), 0.0)
+    hub_dy = jnp.where(y_hub + b1 > 0.0, dot(hub_dz2[:, :OUT], w2t), 0.0)
     db1 = jnp.sum(dy, axis=0, keepdims=True)
     for j, piece in enumerate(split3(dy)):
         dy_s[j, :NODES, :] = piece
@@ -334,9 +334,9 @@
     for piece in split3(hub_back):
         dz1 = dz1 + dot(hub_put, piece)
     dz1_s[...] = dz1.astype(BF16)
-    dw1 = dot(xt_s[:FIN, :], dz1_s[...])
-
-    dx_ref[...] = dot_nt(dz1_s[...], w1_ref[...])
+    dw1 = dot(xt_ref[...], dz1_s[...])
+
+    dxt_ref[...] = dot_nt(w1_ref[...], dz1_s[...])
     for h in range(2):
         a1[h, :FIN, :] = dw1[:, h * 256:(h + 1) * 256]
         a1[h, FIN:, :] = jnp.broadcast_to(db1[:, h * 256:(h + 1) * 256], (8, 256))
@@ -345,8 +345,8 @@
         dw1_ref[:, h * 256:(h + 1) * 256] = tot1[h, :FIN, :]
         db1_ref[:, h * 256:(h + 1) * 256] = tot1[h, FIN:FIN + 1, :]
     for h in range(2):
-        dw2_ref[h * 256:(h + 1) * 256, :] = tot2[h, :256, :OUT]
-    db2_ref[...] = tot2[0, 256:257, :OUT]
+        dw2t_ref[:, h * 256:(h + 1) * 256] = tot2[h, :OUT, :]
+    db2_ref[...] = tot2[0, 112:113, :OUT]
 
 
 def step(hi, mid, lo, x, w1, b1, w2, dh, send, hubs):
@@ -356,7 +356,7 @@
     b16 = lambda *shape: pltpu.VMEM(shape, BF16)
     return pl.pallas_call(
         step_kernel,
-        out_shape=(out(NODES, FIN), out(FIN, HID), out(HID, OUT), out(1, HID), out(1, OUT)),
+        out_shape=(out(FIN, NODES), out(FIN, HID), out(OUT, HID), out(1, HID), out(1, OUT)),
         in_specs=[vmem] * 10,
         out_specs=(vmem,) * 5,
         scratch_shapes=[
@@ -364,8 +364,8 @@
             b16(HID, NODES + HALO), f32(HID, COLS), b16(COLS, 384), f32(NODES, 128), f32(HALO + HUBS, 128),
             f32(4, SEND + HUBS, 128), f32(4, SEND + HUBS, 128), f32(HUBS, HID), f32(4, HUBS, HID),
             b16(3, COLS, HID), f32(NODES, HID), f32(4, SEND + HUBS, HID), f32(4, SEND + HUBS, HID),
-            f32(HALO + HUBS, HID), b16(NODES, HID), b16(FIN + 8, NODES),
-            f32(2, 264, 128), f32(264, 128), f32(2, 264, 128), f32(2, 264, 128),
+            f32(HALO + HUBS, HID), b16(NODES, HID),
+            f32(2, 120, 256), f32(120, 256), f32(2, 120, 256), f32(2, 120, 256),
             f32(2, 208, 256), f32(208, 256), f32(2, 208, 256), f32(2, 208, 256),
             pltpu.SemaphoreType.DMA((24,)), pltpu.SemaphoreType.DMA((24,)),
         ],
@@ -384,8 +384,8 @@
     def device_step(x, dst, src, w, send, hub_ids, w_first, b_first, w_second, dy_out):
         hi, mid, lo = build(hub_ids, dst, src, w)
         dx, dw1, dw2, db1, db2 = step(
-            hi, mid, lo, x, w_first, b_first.reshape(1, HID), w_second, dy_out, send.reshape(1, HALO), hub_ids.reshape(1, HUBS))
-        return dx, dw1, dw2, db1.reshape(HID), db2.reshape(OUT)
+            hi, mid, lo, x.T, w_first, b_first.reshape(1, HID), w_second.T, dy_out.T, send.reshape(1, HALO), hub_ids.reshape(1, HUBS))
+        return dx.T, dw1, dw2.T, db1.reshape(HID), db2.reshape(OUT)
 
     return jax.shard_map(
         device_step,

time: 114 us -> 112 us (0.982)
    unnamed x24 -> x27, local copies, waits for them, and re-layouts: 14.4 us -> 13.4 us
where the time goes in v2:
time: 112 us
  Pallas kernels  97.7 us (87%)
  local copies, waits for them, and re-layouts  13.4 us (12%)
    pallas_call x1, Pallas kernels, step(): pl.pallas_call(step_kernel, out_shape=(out(FIN, NODES), out(FIN, HID), ou...  52.1 us
    pallas_call x1, Pallas kernels, build(): pl.pallas_call(build_kernel, out_shape=(piece,) * 3, in_specs=[pl.BlockSp...  45.6 us
    unnamed x27, local copies, waits for them, and re-layouts  13.4 us

profile of v2, /device:TPU:0, one launch (start us, length us, event | category | flops | bytes accessed | tf_op | source)
XLA Modules:
  0.0 111.8 jit_solution(14850968202141194370)
XLA Ops:
  0.6 0.0 copy-start.5
  0.6 0.8 copy-done.5
  1.5 0.0 copy-start.6
  1.5 0.8 copy-done.6
  2.3 0.0 copy-start.7
  2.3 0.8 copy-done.7
  3.2 0.0 copy-start.8
  3.2 0.7 copy-done.8
  3.8 45.6 %build.1 = (bf16[1296,1152]{1,0:T(8,128)(2,1)S(1)}, bf16[1296,1152]{1,0:T(8,128)(2,1)S(1)}, bf16[1296,1152]{1,0:T(8,128)(2,1)}) custom-call(s32[16]{0:T(128)S(1)} %copy-done.8, s32[128,128]{1,0:T(8,128)S(1)} %bitcast.18, s32[128,128]{1,0:T(8,128)S(1)} %bitcast.19, f32[128,128]{1,0:T(8,128)S(1)} %bitcast.20), custom_call_target="tpu_custom_call" | custom-call | tf_op jit(solution)/shard_map/build/pallas_call | solution.py:106
  49.4 0.0 copy-start
  49.4 1.6 %copy-done = bf16[1296,1152]{1,0:T(8,128)(2,1)} copy-done((bf16[1296,1152]{1,0:T(8,128)(2,1)}, bf16[1296,1152]{1,0:T(8,128)(2,1)S(1)}, u32[]{:S(2)}) %copy-start) | copy-done | bytes 2986008
  51.1 0.0 copy-start.1
  51.1 1.0 copy-done.1
  52.1 0.0 copy-start.2
  52.1 1.0 copy-done.2
  53.1 0.0 copy-start.3
  53.1 0.9 copy-done.3
  54.0 0.0 copy-start.4
  54.0 0.9 copy-done.4
  54.9 0.0 copy-start.9
  54.9 0.7 copy-done.9
  55.6 0.0 copy-start.10
  55.6 0.7 copy-done.10
  56.3 52.1 %step.1 = (f32[200,1024]{1,0:T(8,128)S(1)}, f32[200,512]{1,0:T(8,128)S(1)}, f32[107,512]{1,0:T(8,128)S(1)}, f32[1,512]{1,0:T(1,128)S(1)}, f32[1,107]{1,0:T(1,128)S(1)}) custom-call(bf16[1296,1152]{1,0:T(8,128)(2,1)S(1)} %get-tuple-element.13.hi_ref, bf16[1296,1152]{1,0:T(8,128)(2,1)} %copy-done, bf16[1296,1152]{1,0:T(8,128)(2,1)} %get-tuple-element.15.lo_ref, ...), custom_call_target="tpu_custom_call" | custom-call | tf_op jit(solution)/shard_map/step/pallas_call | solution.py:357
  108.4 0.9 copy.20
  109.3 0.8 copy.21
  110.0 0.7 copy.22
  110.7 0.6 copy.23
  111.3 0.5 copy.24
Async XLA Ops:
  0.6 0.8 copy-start.5
  1.5 0.8 copy-start.6
  2.3 0.8 copy-start.7
  3.2 0.7 copy-start.8
  49.4 1.6 %copy-start = (bf16[1296,1152]{1,0:T(8,128)(2,1)}, bf16[1296,1152]{1,0:T(8,128)(2,1)S(1)}, u32[]{:S(2)}) copy-start(bf16[1296,1152]{1,0:T(8,128)(2,1)S(1)} %get-tuple-element.14.mid_ref) | copy-start | bytes 8957956
  51.1 1.0 copy-start.1
  52.1 1.0 copy-start.2
  53.1 0.9 copy-start.3
  54.0 0.9 copy-start.4
  54.9 0.7 copy-start.9
  55.6 0.7 copy-start.10

commit v3 on v2

--- a/solution.py
+++ b/solution.py
@@ -15,8 +15,11 @@
 ROWS = TILES * TABLE
 EDGES = 16384
 HID, OUT, FIN = 512, 107, 200
+
 ACCS = 4
-UNROLL = 4
+GROUP = 2
+CHUNK = 32
+PARTS = 128 // CHUNK
 NT = (((1,), (1,)), ((), ()))
 
 
@@ -35,7 +38,8 @@
     return lax.dot_general(a, b, NT, preferred_element_type=F32)
 
 
-def build_kernel(hub_ref, dst_ref, src_ref, w_ref, hi_ref, mid_ref, lo_ref, val_ref, row_ref, lane_ref, row_smem, sem, *accs):
+def build_kernel(hub_ref, dst_ref, src_ref, w_ref, hi_ref, mid_ref, lo_ref, row_ref, lane_ref, perm_ref, val_a, val_b, sem, *rest):
+    row_smem, accs = rest[:8], rest[8:]
     base = lax.axis_index("graph") * NODES
     dst, src = dst_ref[...], src_ref[...]
     new_dst, new_src = dst, src
@@ -46,8 +50,12 @@
         new_src = jnp.where(src == local, NODES + HALO + k, new_src)
     row_ref[...] = (new_dst >> 7) * TABLE + new_src
     lane_ref[...] = new_dst & 127
-    copy = pltpu.make_async_copy(row_ref, row_smem, sem)
-    copy.start()
+    copies = []
+    for s in range(8):
+        perm_ref[s] = row_ref[pl.ds(s, 16, stride=8), :]
+    for s in range(8):
+        copies.append(pltpu.make_async_copy(perm_ref.at[s], row_smem[s], sem.at[s]))
+        copies[-1].start()
 
     def zero(i, carry):
         for acc in accs:
@@ -57,33 +65,48 @@
     lax.fori_loop(0, ROWS // 48, zero, 0)
     iota = lax.broadcasted_iota(jnp.int32, (8, 128), 1)
 
-    def prep(g, carry):
-        at = pl.multiple_of(g * 8, 8)
-        lanes, weights = lane_ref[pl.ds(at, 8), :], w_ref[pl.ds(at, 8), :]
-        for c in range(128):
-            hit = jnp.broadcast_to(lanes[:, c:c + 1], (8, 128)) == iota
-            val = jnp.where(hit, jnp.broadcast_to(weights[:, c:c + 1], (8, 128)), 0.0)
-            val_ref[pl.ds(pl.multiple_of(g * 1024 + c * 8, 8), 8), :] = val
+    def wide(block, c):
+        return jnp.broadcast_to(block[:, c:c + 1], (8, 128))
+
+    def prep(n, val_ref):
+        g, k = n // PARTS, n % PARTS
+        at = pl.ds(pl.multiple_of(g * 8, 8), 8)
+        shift = lax.rem(128 - k * CHUNK, 128)
+        lanes, weights, rows = (pltpu.roll(ref[at, :], shift, 1) for ref in (lane_ref, w_ref, row_ref))
+        same = [jnp.where(rows == pltpu.roll(rows, d, 1), 1.0, 0.0) for d in range(1, GROUP)]
+        for c in range(0, CHUNK, GROUP):
+            vals = []
+            for i in range(GROUP):
+                vals.append(jnp.where(wide(lanes, c + i) == iota, wide(weights, c + i), 0.0))
+            for i in range(GROUP):
+                total = vals[i]
+                for j in range(i):
+                    total = total + wide(same[i - j - 1], c + i) * vals[j]
+                val_ref[(c + i) * 8:(c + i + 1) * 8, :] = total
+
+    def scatter(n, val_ref):
+        g, col = n // PARTS, (n % PARTS) * CHUNK
+        for c in range(0, CHUNK, GROUP):
+            for s in range(8):
+                acc = accs[s % ACCS]
+                rows = [row_smem[s][g, col + c + i] for i in range(GROUP)]
+                sums = [acc[pl.ds(rows[i], 1), :] + val_ref[(c + i) * 8 + s:(c + i) * 8 + s + 1, :] for i in range(GROUP)]
+                for r, total in zip(rows, sums):
+                    acc[pl.ds(r, 1), :] = total
+
+    prep(0, val_a)
+    for copy in copies:
+        copy.wait()
+    last = 16 * PARTS - 1
+
+    def turn(h, carry):
+        prep(2 * h + 1, val_b)
+        scatter(2 * h, val_a)
+        prep(jnp.minimum(2 * h + 2, last), val_a)
+        scatter(2 * h + 1, val_b)
         return carry
 
-    lax.fori_loop(0, 16, prep, 0)
-    copy.wait()
-
-    def scatter(t, carry):
-        per_group = 128 // UNROLL
-        group = t // per_group
-        col = (t - group * per_group) * UNROLL
-        vbase = pl.multiple_of(t * UNROLL * 8, 8 * UNROLL)
-        n = 0
-        for c in range(UNROLL):
-            for s in range(8):
-                acc = accs[n % ACCS]
-                n += 1
-                r = row_smem[group * 8 + s, col + c]
-                acc[pl.ds(r, 1), :] = acc[pl.ds(r, 1), :] + val_ref[pl.ds(vbase + c * 8 + s, 1), :]
-        return carry
-
-    lax.fori_loop(0, EDGES // (8 * UNROLL), scatter, 0)
+    lax.fori_loop(0, 8 * PARTS, turn, 0)
 
     def finish(i, carry):
         at = pl.multiple_of(i * 48, 16)
@@ -109,12 +132,13 @@
         in_specs=[pl.BlockSpec(memory_space=pltpu.SMEM)] + [vmem] * 3,
         out_specs=(vmem,) * 3,
         scratch_shapes=[
-            pltpu.VMEM((EDGES, 128), F32),
             pltpu.VMEM((128, 128), jnp.int32),
             pltpu.VMEM((128, 128), jnp.int32),
-            pltpu.SMEM((128, 128), jnp.int32),
-            pltpu.SemaphoreType.DMA,
-        ] + [pltpu.VMEM((ROWS, 128), F32)] * ACCS,
+            pltpu.VMEM((8, 16, 128), jnp.int32),
+            pltpu.VMEM((1024, 128), F32),
+            pltpu.VMEM((1024, 128), F32),
+            pltpu.SemaphoreType.DMA((8,)),
+        ] + [pltpu.SMEM((16, 128), jnp.int32)] * 8 + [pltpu.VMEM((ROWS, 128), F32)] * ACCS,
         compiler_params=pltpu.CompilerParams(vmem_limit_bytes=48 << 20),
         name="build",
     )(hub_ids, square(dst), square(src), square(w))

time: 112 us -> 95.5 us (0.85)
  Pallas kernels: 97.7 us -> 81.5 us
    pallas_call x1, Pallas kernels: 45.6 us -> 28.5 us  [build(): pl.pallas_call(build_kernel, out_shape=(piece,) * 3, in_specs=[pl.BlockSp...]
where the time goes in v3:
time: 95.5 us; the launch traced here: 95.6 us
  Pallas kernels  81.5 us (85%)
  local copies, waits for them, and re-layouts  13.4 us (14%)
    pallas_call x1, Pallas kernels, step(): pl.pallas_call(step_kernel, out_shape=(out(FIN, NODES), out(FIN, HID), ou...  53.1 us
    pallas_call x1, Pallas kernels, build(): pl.pallas_call(build_kernel, out_shape=(piece,) * 3, in_specs=[pl.BlockSp...  28.5 us
    unnamed x27, local copies, waits for them, and re-layouts  13.4 us

profile of v3, /device:TPU:0, one launch (start us, length us, event | category | flops | bytes accessed | tf_op | source)
XLA Modules:
  0.0 95.6 jit_solution(5468392126668500233)
XLA Ops:
  0.6 0.0 copy-start.5
  0.6 0.8 copy-done.5
  1.5 0.0 copy-start.6
  1.5 0.8 copy-done.6
  2.3 0.0 copy-start.7
  2.3 0.8 copy-done.7
  3.2 0.0 copy-start.8
  3.2 0.7 copy-done.8
  3.8 28.5 %build.1 = (bf16[1296,1152]{1,0:T(8,128)(2,1)S(1)}, bf16[1296,1152]{1,0:T(8,128)(2,1)S(1)}, bf16[1296,1152]{1,0:T(8,128)(2,1)}) custom-call(s32[16]{0:T(128)S(1)} %copy-done.8, s32[128,128]{1,0:T(8,128)S(1)} %bitcast.18, s32[128,128]{1,0:T(8,128)S(1)} %bitcast.19, f32[128,128]{1,0:T(8,128)S(1)} %bitcast.20), custom_call_target="tpu_custom_call" | custom-call | tf_op jit(solution)/shard_map/build/pallas_call | solution.py:129
  32.3 0.0 copy-start
  32.3 1.6 %copy-done = bf16[1296,1152]{1,0:T(8,128)(2,1)} copy-done((bf16[1296,1152]{1,0:T(8,128)(2,1)}, bf16[1296,1152]{1,0:T(8,128)(2,1)S(1)}, u32[]{:S(2)}) %copy-start) | copy-done | bytes 2986008
  33.9 0.0 copy-start.1
  33.9 1.0 %copy-done.1 = f32[1024,107]{0,1:T(8,128)S(1)} copy-done((f32[1024,107]{0,1:T(8,128)S(1)}, f32[1024,107]{0,1:T(8,128)}, u32[]{:S(2)}) %copy-start.1) | copy-done | bytes 438296
  34.9 0.0 copy-start.2
  34.9 1.0 %copy-done.2 = bf16[1024,200]{0,1:T(8,128)(2,1)S(1)} copy-done((bf16[1024,200]{0,1:T(8,128)(2,1)S(1)}, bf16[1024,200]{0,1:T(8,128)(2,1)}, u32[]{:S(2)}) %copy-start.2) | copy-done | bytes 409624
  35.9 0.0 copy-start.3
  35.9 0.9 copy-done.3
  36.8 0.0 copy-start.4
  36.8 0.9 copy-done.4
  37.7 0.0 copy-start.9
  37.7 0.7 copy-done.9
  38.4 0.0 copy-start.10
  38.4 0.7 copy-done.10
  39.1 53.1 %step.1 = (f32[200,1024]{1,0:T(8,128)S(1)}, f32[200,512]{1,0:T(8,128)S(1)}, f32[107,512]{1,0:T(8,128)S(1)}, f32[1,512]{1,0:T(1,128)S(1)}, f32[1,107]{1,0:T(1,128)S(1)}) custom-call(bf16[1296,1152]{1,0:T(8,128)(2,1)S(1)} %get-tuple-element.13.hi_ref, bf16[1296,1152]{1,0:T(8,128)(2,1)} %copy-done, bf16[1296,1152]{1,0:T(8,128)(2,1)} %get-tuple-element.15.lo_ref, ...), custom_call_target="tpu_custom_call" | custom-call | tf_op jit(solution)/shard_map/step/pallas_call | solution.py:381
  92.2 0.9 copy.20
  93.1 0.8 copy.21
  93.8 0.7 copy.22
  94.5 0.6 copy.23
  95.1 0.5 copy.24
Async XLA Ops:
  0.6 0.8 copy-start.5
  1.5 0.8 copy-start.6
  2.3 0.8 copy-start.7
  3.2 0.7 copy-start.8
  32.3 1.6 %copy-start = (bf16[1296,1152]{1,0:T(8,128)(2,1)}, bf16[1296,1152]{1,0:T(8,128)(2,1)S(1)}, u32[]{:S(2)}) copy-start(bf16[1296,1152]{1,0:T(8,128)(2,1)S(1)} %get-tuple-element.14.mid_ref) | copy-start | bytes 8957956
  33.9 1.0 %copy-start.1 = (f32[1024,107]{0,1:T(8,128)S(1)}, f32[1024,107]{0,1:T(8,128)}, u32[]{:S(2)}) copy-start(f32[1024,107]{0,1:T(8,128)} %param.19) | copy-start | bytes 1314820
  34.9 1.0 %copy-start.2 = (bf16[1024,200]{0,1:T(8,128)(2,1)S(1)}, bf16[1024,200]{0,1:T(8,128)(2,1)}, u32[]{:S(2)}) copy-start(bf16[1024,200]{0,1:T(8,128)(2,1)} %param.10) | copy-start | bytes 1228804
  35.9 0.9 copy-start.3
  36.8 0.9 copy-start.4
  37.7 0.7 copy-start.9
  38.4 0.7 copy-start.10

commit v4 on v3

v4 whole, which is shorter than its diff:
```python
import functools

import jax
import jax.numpy as jnp
from jax import lax
from jax.experimental import pallas as pl
from jax.experimental.pallas import tpu as pltpu
from jax.sharding import PartitionSpec as P

F32, BF16 = jnp.float32, jnp.bfloat16
NODES, SEND, HALO, HUBS = 1024, 64, 256, 16
TABLE = NODES + HALO + HUBS
TILES = 9
COLS = TILES * 128
ROWS = TILES * TABLE
EDGES = 16384
HID, OUT, FIN = 512, 107, 200

ACCS = 4
GROUP = 2
CHUNK = 32
PARTS = 128 // CHUNK
BUILD_VMEM = 27 << 20
STEP_VMEM = 34 << 20
NT = (((1,), (1,)), ((), ()))


def split3(x):
    hi = x.astype(BF16)
    rest = x - hi.astype(F32)
    mid = rest.astype(BF16)
    return hi, mid, (rest - mid.astype(F32)).astype(BF16)


def dot(a, b):
    return jnp.dot(a, b, preferred_element_type=F32)


def dot_nt(a, b):
    return lax.dot_general(a, b, NT, preferred_element_type=F32)


def build_kernel(hub_hbm, dst_hbm, src_hbm, w_hbm, hi_ref, mid_ref, lo_ref, hub_ref, dst_ref, src_ref, w_ref, row_ref, lane_ref, perm_ref, val_a, val_b, sem, *rest):
    row_smem, accs = rest[:8], rest[8:]
    loads = []
    for i, (a, b) in enumerate(((hub_hbm, hub_ref), (dst_hbm, dst_ref), (src_hbm, src_ref), (w_hbm, w_ref))):
        loads.append(pltpu.make_async_copy(a, b, sem.at[8 + i]))
        loads[-1].start()

    def zero(i, carry):
        for acc in accs:
            acc[pl.ds(pl.multiple_of(i * 48, 8), 48), :] = jnp.zeros((48, 128), F32)
        return carry

    lax.fori_loop(0, ROWS // 48, zero, 0)
    for load in loads:
        load.wait()
    base = lax.axis_index("graph") * NODES
    dst, src = dst_ref[...], src_ref[...]
    new_dst, new_src = dst, src
    for k in range(HUBS):
        local = hub_ref[k] - base
        local = jnp.where((local >= 0) & (local < NODES), local, -1)
        new_dst = jnp.where(dst == local, NODES + k, new_dst)
        new_src = jnp.where(src == local, NODES + HALO + k, new_src)
    row_ref[...] = (new_dst >> 7) * TABLE + new_src
    lane_ref[...] = new_dst & 127
    copies = []
    for s in range(8):
        perm_ref[s] = row_ref[pl.ds(s, 16, stride=8), :]
    for s in range(8):
        copies.append(pltpu.make_async_copy(perm_ref.at[s], row_smem[s], sem.at[s]))
        copies[-1].start()

    iota = lax.broadcasted_iota(jnp.int32, (8, 128), 1)

    def wide(block, c):
        return jnp.broadcast_to(block[:, c:c + 1], (8, 128))

    def prep(n, val_ref):
        g, k = n // PARTS, n % PARTS
        at = pl.ds(pl.multiple_of(g * 8, 8), 8)
        shift = lax.rem(128 - k * CHUNK, 128)
        lanes, weights, rows = (pltpu.roll(ref[at, :], shift, 1) for ref in (lane_ref, w_ref, row_ref))
        same = [jnp.where(rows == pltpu.roll(rows, d, 1), 1.0, 0.0) for d in range(1, GROUP)]
        for c in range(0, CHUNK, GROUP):
            vals = []
            for i in range(GROUP):
                vals.append(jnp.where(wide(lanes, c + i) == iota, wide(weights, c + i), 0.0))
            for i in range(GROUP):
                total = vals[i]
                for j in range(i):
                    total = total + wide(same[i - j - 1], c + i) * vals[j]
                val_ref[(c + i) * 8:(c + i + 1) * 8, :] = total

    def scatter(n, val_ref):
        g, col = n // PARTS, (n % PARTS) * CHUNK
        for c in range(0, CHUNK, GROUP):
            for s in range(8):
                acc = accs[s % ACCS]
                rows = [row_smem[s][g, col + c + i] for i in range(GROUP)]
                sums = [acc[pl.ds(rows[i], 1), :] + val_ref[(c + i) * 8 + s:(c + i) * 8 + s + 1, :] for i in range(GROUP)]
                for r, total in zip(rows, sums):
                    acc[pl.ds(r, 1), :] = total

    prep(0, val_a)
    for copy in copies:
        copy.wait()
    last = 16 * PARTS - 1

    def turn(h, carry):
        prep(2 * h + 1, val_b)
        scatter(2 * h, val_a)
        prep(jnp.minimum(2 * h + 2, last), val_a)
        scatter(2 * h + 1, val_b)
        return carry

    lax.fori_loop(0, 8 * PARTS, turn, 0)

    def finish(i, carry):
        at = pl.multiple_of(i * 48, 16)
        for t in range(TILES):
            part = pl.ds(pl.multiple_of(t * TABLE + i * 48, 8), 48)
            total = accs[0][part, :]
            for acc in accs[1:]:
                total = total + acc[part, :]
            for piece, ref in zip(split3(total), (hi_ref, mid_ref, lo_ref)):
                ref[pl.ds(at, 48), t * 128:(t + 1) * 128] = piece
        return carry

    lax.fori_loop(0, TABLE // 48, finish, 0)


def build(hub_ids, dst, src, w):
    piece = jax.ShapeDtypeStruct((TABLE, COLS), BF16)
    square = lambda a: a.reshape(128, 128)
    table = pltpu.VMEM((128, 128), jnp.int32)
    return pl.pallas_call(
        build_kernel,
        out_shape=(piece,) * 3,
        in_specs=[pl.BlockSpec(memory_space=pltpu.HBM)] * 4,
        out_specs=(pl.BlockSpec(memory_space=pltpu.VMEM),) * 3,
        scratch_shapes=[
            pltpu.SMEM((HUBS,), jnp.int32), table, table, pltpu.VMEM((128, 128), F32), table, table,
            pltpu.VMEM((8, 16, 128), jnp.int32), pltpu.VMEM((CHUNK * 8, 128), F32), pltpu.VMEM((CHUNK * 8, 128), F32),
            pltpu.SemaphoreType.DMA((12,)),
        ] + [pltpu.SMEM((16, 128), jnp.int32)] * 8 + [pltpu.VMEM((ROWS, 128), F32)] * ACCS,
        compiler_params=pltpu.CompilerParams(vmem_limit_bytes=BUILD_VMEM),
        name="build",
    )(hub_ids, square(dst), square(src), square(w))


def step_kernel(
    hi_ref, mid_ref, lo_ref, xt_hbm, w1_hbm, b1_hbm, w2t_hbm, dht_hbm, send_hbm, hub_hbm,
    dxt_ref, dw1_ref, dw2t_ref, db1_ref, db2_ref,
    xt_ref, w1_ref, b1_ref, w2t_ref, dht_ref, send_ref, hub_ref,
    row_s, pt_s, xs, xr, hs, hr, z_s, yt_s, d2_s, dhub_s, g2_s, g2h_s, rb, sb, ys, yr, dy_s, g1_s, sd, rd, dz1_s,
    a2, half2, got2, tot2, a1, half1, got1, tot1, load_sem, send_sem, recv_sem,
):
    me = lax.axis_index("graph")
    sibling = me + 1 - 2 * lax.rem(me, 2)
    across = lax.rem(me + 2, 4)
    core = lax.rem(me, 2)
    mesh_id = pl.DeviceIdType.MESH
    peers = [lax.rem(me + d, 4) for d in (1, 2, 3)]
    loads = []
    for i, (a, b) in enumerate((
            (send_hbm, send_ref), (hub_hbm, hub_ref), (xt_hbm, xt_ref), (dht_hbm, dht_ref), (w1_hbm, w1_ref), (b1_hbm, b1_ref),
            (w2t_hbm, w2t_ref))):
        loads.append(pltpu.make_async_copy(a, b, load_sem.at[i]))
        loads[-1].start()
    barrier = pltpu.get_barrier_semaphore()
    for q in peers:
        pl.semaphore_signal(barrier, inc=1, device_id={"graph": q}, device_id_type=mesh_id)
    for load in loads:
        load.wait()
    pl.semaphore_wait(barrier, 3)
    used = [0]

    def remote(src, dst, q):
        i = used[0]
        used[0] += 1
        copy = pltpu.make_async_remote_copy(
            src_ref=src, dst_ref=dst, send_sem=send_sem.at[i], recv_sem=recv_sem.at[i],
            device_id={"graph": q}, device_id_type=mesh_id)
        copy.start()
        return copy

    def wait_all(copies):
        for copy in copies:
            copy.wait()

    pieces = (hi_ref, mid_ref, lo_ref)
    row_s[...] = jnp.full((1, 384), -1.0, F32)
    row_s[:, :HALO] = send_ref[...].astype(F32)
    hub_local = hub_ref[...] - me * NODES
    row_s[:, HALO:HALO + HUBS] = jnp.where((hub_local >= 0) & (hub_local < NODES), hub_local, -1).astype(F32)
    row = row_s[...]
    column = jnp.transpose(jnp.broadcast_to(row, (128, 384)))
    lane = lax.broadcasted_iota(jnp.int32, (272, 128), 1).astype(F32)
    picks = jnp.concatenate(
        [jnp.where(column[:272] == lane + float(j * 128), 1.0, 0.0).astype(BF16) for j in range(8)], axis=1)
    xt = xt_ref[...]
    sent = dot_nt(picks, xt).astype(BF16)
    hub_col = column[HALO:HALO + HUBS]
    alias = [jnp.where((hub_col == row[:, j * 128:(j + 1) * 128]) & (hub_col >= 0.0), 1.0, 0.0) for j in range(2)]
    for q in range(4):
        xs[q, :SEND, :] = sent[q * SEND:(q + 1) * SEND]
        xs[q, SEND:SEND + HUBS, :] = sent[HALO:]
        part = alias[q // 2][:, (q % 2) * SEND:(q % 2 + 1) * SEND]
        xs[q, SEND + HUBS:, :SEND] = part.astype(BF16)
        xs[q, SEND + HUBS:, SEND:] = jnp.zeros((HUBS, FIN - SEND), BF16)
    xr[me] = jnp.zeros((96, FIN), BF16)
    dht = dht_ref[...]
    dh = jnp.transpose(jnp.concatenate([dht, jnp.zeros((128 - OUT, NODES), F32)], axis=0))
    for j, piece in enumerate(split3(dh)):
        d2_s[:, j * 128:(j + 1) * 128] = piece
    round_a = [remote(xs.at[q], xr.at[me], q) for q in peers]
    hub_dh = dot(picks[HALO:], d2_s[...])
    hs[...] = (hub_dh[:, :128] + hub_dh[:, 128:256]) + hub_dh[:, 256:]
    hr[me] = hs[...]
    db2 = jnp.sum(dh, axis=0, keepdims=True)
    round_a += [remote(hs, hr.at[me], q) for q in peers]
    sub = lax.broadcasted_iota(jnp.int32, (NODES, 384), 0).astype(F32)
    pt_s[...] = jnp.where(sub == row, 1.0, 0.0).astype(BF16)

    def grad2(rows, cols, right):
        a = dot(hi_ref[rows, cols], right[:, :256])
        b = dot(mid_ref[rows, cols], right[:, :256])
        c = dot(hi_ref[rows, cols], right[:, 256:]) + dot(lo_ref[rows, cols], right[:, :128])
        return ((c + b[:, 128:]) + (a[:, 128:] + b[:, :128])) + a[:, :128]

    own_cols, hub_cols = pl.ds(0, NODES), pl.ds(NODES, 128)
    far_rows = pl.ds(NODES, HALO + HUBS)
    g2h_s[...] = grad2(far_rows, own_cols, d2_s)

    def grad2_own(m, carry):
        at = pl.ds(pl.multiple_of(m * 256, 256), 256)
        g2_s[at, :] = grad2(at, own_cols, d2_s)
        return carry

    lax.fori_loop(0, 4, grad2_own, 0)
    w1t = jnp.transpose(jnp.concatenate([w1_ref[...], jnp.zeros((56, HID), BF16)], axis=0).astype(F32)).astype(BF16)[:, :FIN]
    z_s[:, :NODES] = dot(w1t, xt).astype(BF16)

    def forward_own(at):
        z = z_s[:, :NODES]
        acc = dot(z, hi_ref[:NODES, at])
        acc = acc + dot(z, mid_ref[:NODES, at])
        yt_s[:, at] = acc + dot(z, lo_ref[:NODES, at])

    def over_columns(body):
        def turn(n, carry):
            body(pl.ds(pl.multiple_of(n * 256, 256), 256))
            return carry

        lax.fori_loop(0, 4, turn, 0)

    forward_own(hub_cols)
    wait_all(round_a)

    halo_x = jnp.concatenate([xr[q, :SEND, :] for q in range(4)], axis=0)
    hub_x = sent[HALO:].astype(F32)
    for q in range(4):
        hub_x = hub_x + xr[q, SEND:SEND + HUBS, :].astype(F32)
    z_s[:, NODES:] = dot_nt(w1t, halo_x).astype(BF16)
    z_hub = dot_nt(w1t, hub_x.astype(BF16)).astype(BF16)

    def forward_far(at):
        z = z_s[:, NODES:]
        acc = yt_s[:, at]
        for ref in pieces:
            acc = acc + dot(z, ref[NODES:NODES + HALO, at])
        for ref in pieces:
            acc = acc + dot(z_hub, ref[NODES + HALO:, at])
        yt_s[:, at] = acc

    forward_far(hub_cols)
    ys[...] = jnp.transpose(yt_s[:, NODES:])[:HUBS]
    yr[me] = ys[...]
    hub_dh = (hr[0] + hr[1]) + (hr[2] + hr[3])
    for j, piece in enumerate(split3(hub_dh)):
        dhub_s[:HUBS, j * 128:(j + 1) * 128] = piece
    dhub_s[HUBS:, :] = jnp.zeros((128 - HUBS, 384), BF16)
    round_b = [remote(ys, yr.at[me], q) for q in peers]
    g2h_s[...] += grad2(far_rows, hub_cols, dhub_s)
    far = g2h_s[:HALO, :]
    alias_row = jnp.concatenate([xr[q, SEND + HUBS:, :SEND] for q in range(4)], axis=1)
    hub_g2 = g2h_s[HALO:, :]
    for piece in split3(far):
        hub_g2 = hub_g2 + dot(alias_row, piece)
    for q in range(4):
        sb[q, :SEND, :] = far[q * SEND:(q + 1) * SEND]
        sb[q, SEND:, :] = hub_g2
    rb[me] = sb[me]
    round_b += [remote(sb.at[q], rb.at[me], q) for q in peers]

    over_columns(forward_own)
    over_columns(forward_far)

    def grad2_hub(m, carry):
        at = pl.ds(pl.multiple_of(m * 256, 256), 256)
        g2_s[at, :] += grad2(at, hub_cols, dhub_s)
        return carry

    lax.fori_loop(0, 4, grad2_hub, 0)
    wait_all(round_b)

    hub_dz2 = ((rb[0, SEND:, :] + rb[1, SEND:, :]) + (rb[2, SEND:, :] + rb[3, SEND:, :])).astype(BF16)
    keep = lax.broadcasted_iota(jnp.int32, (4, SEND, 128), 0) != me
    back = jnp.where(keep, rb[:, :SEND, :], 0.0).reshape(HALO, 128)
    own = g2_s[...]
    halo_pick = pt_s[:, :HALO]
    hub_put = pt_s[:, HALO:HALO + HUBS]
    for piece in split3(back):
        own = own + dot(halo_pick, piece)
    is_hub = dot(hub_put, jnp.ones((HUBS, 128), BF16)) > 0.5
    dz2 = jnp.where(is_hub, dot(hub_put, hub_dz2), own).astype(BF16)

    y_hub = (yr[0] + yr[1]) + (yr[2] + yr[3])
    b1 = b1_ref[...]
    b1_col = jnp.transpose(jnp.broadcast_to(b1, (128, HID)))
    for piece in split3(jnp.transpose(jnp.concatenate([y_hub, jnp.zeros((112, HID), F32)], axis=0))):
        yt_s[:, :NODES] += dot(piece[:, :HUBS], picks[HALO:])
    pre = yt_s[:, :NODES] + jnp.concatenate([b1_col] * 8, axis=1)
    yt_s[:, :NODES] = pre
    live = jnp.transpose(jnp.where(pre > 0.0, 1.0, 0.0))
    w2t = w2t_ref[...]
    dy = jnp.where(live > 0.5, dot(dz2[:, :OUT], w2t), 0.0)
    hub_dy = jnp.where(y_hub + b1 > 0.0, dot(hub_dz2[:, :OUT], w2t), 0.0)
    db1 = jnp.sum(dy, axis=0, keepdims=True)
    for j, piece in enumerate(split3(dy)):
        dy_s[j, :NODES, :] = piece
    for j, piece in enumerate(split3(hub_dy)):
        dy_s[j, NODES:NODES + HUBS, :] = piece
        dy_s[j, NODES + HUBS:, :] = jnp.zeros((112, HID), BF16)

    class GroupSum:
        def __init__(self, own, half, got, total):
            self.own, self.half, self.got, self.total = own, half, got, total
            self.copy = remote(own.at[1 - core], got.at[0], sibling)

        def across(self):
            self.copy.wait()
            self.half[...] = self.own[core] + self.got[0]
            self.copy = remote(self.half, self.got.at[1], across)

        def back(self):
            self.copy.wait()
            self.total[core] = self.half[...] + self.got[1]
            self.copy = remote(self.total.at[core], self.total.at[core], sibling)

        def done(self):
            self.copy.wait()

    def grad1(rows, cols):
        acc = dot(lo_ref[rows, :], dy_s[0, :, cols])
        acc = acc + dot(mid_ref[rows, :], dy_s[1, :, cols])
        acc = acc + dot(hi_ref[rows, :], dy_s[2, :, cols])
        acc = acc + dot(mid_ref[rows, :], dy_s[0, :, cols])
        acc = acc + dot(hi_ref[rows, :], dy_s[1, :, cols])
        return acc + dot(hi_ref[rows, :], dy_s[0, :, cols])

    halves = (pl.ds(0, 256), pl.ds(256, 256))
    round_d = []
    for h, cols in enumerate(halves):
        ret = grad1(far_rows, cols)
        for q in range(4):
            sd[h, q, :SEND, :] = ret[q * SEND:(q + 1) * SEND]
            sd[h, q, SEND:, :] = ret[HALO:]
        rd[h, me] = sd[h, me]
        round_d.append([remote(sd.at[h, q], rd.at[h, me], q) for q in peers])

    dw2t = jnp.transpose(dot(jnp.maximum(yt_s[:, :NODES], 0.0).astype(BF16), dz2))
    for h in range(2):
        a2[h, :112, :] = dw2t[:112, h * 256:(h + 1) * 256]
        a2[h, 112:, :128] = jnp.broadcast_to(db2, (8, 128))
        a2[h, 112:, 128:] = jnp.zeros((8, 128), F32)

    def grad1_own(h, m):
        rows = pl.ds(m * 512, 512)
        g1_s[rows, halves[h]] = grad1(rows, halves[h])

    def finish(h):
        wait_all(round_d[h])
        cols = halves[h]
        keep = lax.broadcasted_iota(jnp.int32, (4, SEND, 256), 0) != me
        back = jnp.where(keep, rd[h, :, :SEND, :], 0.0).reshape(HALO, 256)
        hub_back = (rd[h, 0, SEND:, :] + rd[h, 1, SEND:, :]) + (rd[h, 2, SEND:, :] + rd[h, 3, SEND:, :])
        dz1 = g1_s[:, cols]
        for piece in split3(back):
            dz1 = dz1 + dot(halo_pick, piece)
        for piece in split3(hub_back):
            dz1 = dz1 + dot(hub_put, piece)
        dz1 = dz1.astype(BF16)
        dz1_s[:, cols] = dz1
        dw1 = dot(xt_ref[...], dz1)
        for i in range(2):
            at = slice(i * 128, (i + 1) * 128)
            a1[h, i, :FIN, :] = dw1[:, at]
            a1[h, i, FIN:, :] = jnp.broadcast_to(db1[:, h * 256 + i * 128:h * 256 + (i + 1) * 128], (8, 128))
        return GroupSum(a1.at[h], half1.at[h], got1.at[h], tot1.at[h])

    sum2 = GroupSum(a2, half2, got2, tot2)
    grad1_own(0, 0)
    sum2.across()
    grad1_own(0, 1)
    sum1 = [finish(0)]
    grad1_own(1, 0)
    sum1[0].across()
    sum2.back()
    grad1_own(1, 1)
    sum1.append(finish(1))
    sum1[0].back()
    sum2.done()
    for h in range(2):
        dw2t_ref[:, h * 256:(h + 1) * 256] = tot2[h, :OUT, :]
    db2_ref[...] = tot2[0, 112:113, :OUT]
    sum1[1].across()
    dxt_ref[...] = dot_nt(w1_ref[...], dz1_s[...])
    sum1[1].back()
    sum1[0].done()

    def put(h):
        for i in range(2):
            at = slice(h * 256 + i * 128, h * 256 + (i + 1) * 128)
            dw1_ref[:, at] = tot1[h, i, :FIN, :]
            db1_ref[:, at] = tot1[h, i, FIN:FIN + 1, :]

    put(0)
    sum1[1].done()
    put(1)


def step(hi, mid, lo, xt, w1, b1, w2t, dht, send, hubs):
    vmem = pl.BlockSpec(memory_space=pltpu.VMEM)
    out = lambda *shape: jax.ShapeDtypeStruct(shape, F32)
    f32 = lambda *shape: pltpu.VMEM(shape, F32)
    b16 = lambda *shape: pltpu.VMEM(shape, BF16)
    return pl.pallas_call(
        step_kernel,
        out_shape=(out(FIN, NODES), out(FIN, HID), out(OUT, HID), out(1, HID), out(1, OUT)),
        in_specs=[vmem] * 3 + [pl.BlockSpec(memory_space=pltpu.HBM)] * 7,
        out_specs=(vmem,) * 5,
        scratch_shapes=[
            b16(FIN, NODES), b16(FIN, HID), f32(1, HID), b16(OUT, HID), f32(OUT, NODES),
            pltpu.VMEM((1, HALO), jnp.int32), pltpu.VMEM((1, HUBS), jnp.int32),
            f32(1, 384), b16(NODES, 384), b16(4, 96, FIN), b16(4, 96, FIN), f32(HUBS, 128), f32(4, HUBS, 128),
            b16(HID, NODES + HALO), f32(HID, COLS), b16(NODES, 384), b16(128, 384), f32(NODES, 128), f32(HALO + HUBS, 128),
            f32(4, SEND + HUBS, 128), f32(4, SEND + HUBS, 128), f32(HUBS, HID), f32(4, HUBS, HID),
            b16(3, COLS, HID), f32(NODES, HID), f32(2, 4, SEND + HUBS, 256), f32(2, 4, SEND + HUBS, 256), b16(NODES, HID),
            f32(2, 120, 256), f32(120, 256), f32(2, 120, 256), f32(2, 120, 256),
            f32(2, 2, 208, 128), f32(2, 208, 128), f32(2, 2, 208, 128), f32(2, 2, 208, 128),
            pltpu.SemaphoreType.DMA((7,)), pltpu.SemaphoreType.DMA((28,)), pltpu.SemaphoreType.DMA((28,)),
        ],
        compiler_params=pltpu.CompilerParams(collective_id=0, has_side_effects=True, vmem_limit_bytes=STEP_VMEM),
        name="step",
    )(hi, mid, lo, xt, w1, b1, w2t, dht, send, hubs)


def emit_kernel(*refs):
    ins, outs, sem = refs[:5], refs[5:10], refs[10]
    copies = [pltpu.make_async_copy(a, b, sem.at[i]) for i, (a, b) in enumerate(zip(ins, outs))]
    for copy in copies:
        copy.start()
    for copy in copies:
        copy.wait()


def emit(*arrays):
    return pl.pallas_call(
        emit_kernel,
        out_shape=tuple(jax.ShapeDtypeStruct(a.shape, a.dtype) for a in arrays),
        in_specs=[pl.BlockSpec(memory_space=pltpu.VMEM)] * 5,
        out_specs=(pl.BlockSpec(memory_space=pltpu.HBM),) * 5,
        scratch_shapes=[pltpu.SemaphoreType.DMA((5,))],
        compiler_params=pltpu.CompilerParams(vmem_limit_bytes=4 << 20),
        name="emit",
    )(*arrays)


def solution(mesh):
    vertex_spec = P(("data", "graph"))
    vertex_rows = P(("data", "graph"), None)
    part_spec = P("data")
    part_rows = P("data", None)
    replicated = P()

    def device_step(x, dst, src, w, send, hub_ids, w_first, b_first, w_second, dy_out):
        hi, mid, lo = build(hub_ids, dst, src, w)
        dx, dw1, dw2, db1, db2 = emit(*step(
            hi, mid, lo, x.T, w_first, b_first.reshape(1, HID), w_second.T, dy_out.T, send.reshape(1, HALO), hub_ids.reshape(1, HUBS)))
        return dx.T, dw1, dw2.T, db1.reshape(HID), db2.reshape(OUT)

    return jax.shard_map(
        device_step,
        mesh=mesh,
        in_specs=(vertex_rows, vertex_spec, vertex_spec, vertex_spec, vertex_spec, part_spec, replicated, replicated, replicated, vertex_rows),
        out_specs=(vertex_rows, part_rows, part_rows, part_spec, part_spec),
        check_vma=False,
    )
```

time: 95.5 us -> 95 us (level); the launches traced: 95.6 us -> 93.7 us
  local copies, waits for them, and re-layouts: 13.4 us -> 9.02 us
  Pallas kernels: 81.5 us -> 83.8 us
    unnamed x27 -> x22, local copies, waits for them, and re-layouts: 13.4 us -> 9.02 us
    pallas_call x1, Pallas kernels: 53.1 us -> 56.4 us  [step(): pl.pallas_call(step_kernel, out_shape=(out(FIN, NODES), out(FIN, HID), ou...]
    pallas_call x1, Pallas kernels: 28.5 us -> 26.3 us  [build(): pl.pallas_call(build_kernel, out_shape=(piece,) * 3, in_specs=[pl.BlockSp...]
    pallas_call x0 -> x1, Pallas kernels: none -> 1.14 us  [emit(): pl.pallas_call(emit_kernel, out_shape=tuple((jax.ShapeDtypeStruct(a.shape...]
where the time goes in v4:
time: 95 us; the launch traced here: 93.7 us
  Pallas kernels  83.8 us (88%)
  local copies, waits for them, and re-layouts  9.02 us (9%)
    pallas_call x1, Pallas kernels, step(): pl.pallas_call(step_kernel, out_shape=(out(FIN, NODES), out(FIN, HID), ou...  56.4 us
    pallas_call x1, Pallas kernels, build(): pl.pallas_call(build_kernel, out_shape=(piece,) * 3, in_specs=[pl.BlockSp...  26.3 us
    unnamed x22, local copies, waits for them, and re-layouts  9.02 us

profile of v4, /device:TPU:0, one launch (start us, length us, event | category | flops | bytes accessed | tf_op | source)
XLA Modules:
  0.0 93.7 jit_solution(12735255949122859660)
XLA Ops:
  0.6 0.0 copy-start.4
  0.6 0.8 copy-done.4
  1.5 0.0 copy-start.5
  1.5 0.8 copy-done.5
  2.3 0.0 copy-start.6
  2.3 0.8 copy-done.6
  3.2 0.0 copy-start.7
  3.2 0.7 copy-done.7
  3.8 26.3 %build.1 = (bf16[1296,1152]{1,0:T(8,128)(2,1)S(1)}, bf16[1296,1152]{1,0:T(8,128)(2,1)S(1)}, bf16[1296,1152]{1,0:T(8,128)(2,1)S(1)}) custom-call(s32[16]{0:T(128)S(1)} %copy-done.7, s32[128,128]{1,0:T(8,128)S(1)} %bitcast.16, s32[128,128]{1,0:T(8,128)S(1)} %bitcast.17, f32[128,128]{1,0:T(8,128)S(1)} %bitcast.18), custom_call_target="tpu_custom_call" | custom-call | tf_op jit(solution)/shard_map/build/pallas_call | solution.py:138
  30.1 0.0 copy-start
  30.2 1.0 %copy-done = f32[1024,107]{0,1:T(8,128)S(1)} copy-done((f32[1024,107]{0,1:T(8,128)S(1)}, f32[1024,107]{0,1:T(8,128)}, u32[]{:S(2)}) %copy-start) | copy-done | bytes 438296
  31.2 0.0 copy-start.1
  31.2 1.0 %copy-done.1 = bf16[1024,200]{0,1:T(8,128)(2,1)S(1)} copy-done((bf16[1024,200]{0,1:T(8,128)(2,1)S(1)}, bf16[1024,200]{0,1:T(8,128)(2,1)}, u32[]{:S(2)}) %copy-start.1) | copy-done | bytes 409624
  32.2 0.0 copy-start.2
  32.2 0.9 copy-done.2
  33.1 0.0 copy-start.3
  33.1 0.9 copy-done.3
  34.0 0.0 copy-start.8
  34.0 0.7 copy-done.8
  34.6 0.0 copy-start.9
  34.7 0.7 copy-done.9
  35.3 0.0 copy-start.10
  35.3 0.7 copy-done.10
  36.0 56.4 %step.1 = (f32[200,1024]{1,0:T(8,128)S(1)}, f32[200,512]{1,0:T(8,128)S(1)}, f32[107,512]{1,0:T(8,128)S(1)}, f32[1,512]{1,0:T(1,128)S(1)}, f32[1,107]{1,0:T(1,128)S(1)}) custom-call(bf16[1296,1152]{1,0:T(8,128)(2,1)S(1)} %get-tuple-element.18.hi_ref, bf16[1296,1152]{1,0:T(8,128)(2,1)S(1)} %get-tuple-element.19.mid_ref, ...), custom_call_target="tpu_custom_call" | custom-call | tf_op jit(solution)/shard_map/step/pallas_call | solution.py:440
  92.4 1.1 %emit.1 = (f32[200,1024]{1,0:T(8,128)}, f32[200,512]{1,0:T(8,128)}, f32[107,512]{1,0:T(8,128)}, f32[1,512]{1,0:T(1,128)}, f32[1,107]{1,0:T(1,128)}) custom-call(f32[200,1024]{1,0:T(8,128)S(1)} %get-tuple-element.21.refs_0_, f32[200,512]{1,0:T(8,128)S(1)} %get-tuple-element.22.refs_1_, f32[107,512]{1,0:T(8,128)S(1)} %get-tuple-element.23.refs_2_, ...), custom_call_target="tpu_custom_call" | custom-call | tf_op jit(solution)/shard_map/emit/pallas_call | solution.py:471
Async XLA Ops:
  0.6 0.8 copy-start.4
  1.5 0.8 copy-start.5
  2.3 0.8 copy-start.6
  3.2 0.7 copy-start.7
  30.1 1.0 %copy-start = (f32[1024,107]{0,1:T(8,128)S(1)}, f32[1024,107]{0,1:T(8,128)}, u32[]{:S(2)}) copy-start(f32[1024,107]{0,1:T(8,128)} %param.19) | copy-start | bytes 1314820
  31.2 1.0 %copy-start.1 = (bf16[1024,200]{0,1:T(8,128)(2,1)S(1)}, bf16[1024,200]{0,1:T(8,128)(2,1)}, u32[]{:S(2)}) copy-start(bf16[1024,200]{0,1:T(8,128)(2,1)} %param.10) | copy-start | bytes 1228804
  32.2 0.9 copy-start.2
  33.1 0.9 copy-start.3
  34.0 0.7 copy-start.8
  34.6 0.7 copy-start.9
  35.3 0.7 copy-start.10

commit v5 on v4

--- a/solution.py
+++ b/solution.py
@@ -30,6 +30,10 @@
     rest = x - hi.astype(F32)
     mid = rest.astype(BF16)
     return hi, mid, (rest - mid.astype(F32)).astype(BF16)
+
+
+def in_hbm(a):
+    return pltpu.with_memory_space_constraint(a, pltpu.HBM)
 
 
 def dot(a, b):
@@ -147,7 +151,7 @@
         ] + [pltpu.SMEM((16, 128), jnp.int32)] * 8 + [pltpu.VMEM((ROWS, 128), F32)] * ACCS,
         compiler_params=pltpu.CompilerParams(vmem_limit_bytes=BUILD_VMEM),
         name="build",
-    )(hub_ids, square(dst), square(src), square(w))
+    )(*(in_hbm(a) for a in (hub_ids, square(dst), square(src), square(w))))
 
 
 def step_kernel(
@@ -455,7 +459,7 @@
         ],
         compiler_params=pltpu.CompilerParams(collective_id=0, has_side_effects=True, vmem_limit_bytes=STEP_VMEM),
         name="step",
-    )(hi, mid, lo, xt, w1, b1, w2t, dht, send, hubs)
+    )(hi, mid, lo, *(in_hbm(a) for a in (xt, w1, b1, w2t, dht, send, hubs)))
 
 
 def emit_kernel(*refs):

time: 95 us -> 85.3 us (0.90); the launches traced: 93.7 us -> 85 us
  local copies, waits for them, and re-layouts: 9.02 us -> 0 us
    unnamed x22 -> x0, local copies, waits for them, and re-layouts: 9.02 us -> none
where the time goes in v5:
time: 85.3 us; the launch traced here: 85 us
  Pallas kernels  84.2 us (99%)
    pallas_call x1, Pallas kernels, step(): pl.pallas_call(step_kernel, out_shape=(out(FIN, NODES), out(FIN, HID), ou...  56.9 us
    pallas_call x1, Pallas kernels, build(): pl.pallas_call(build_kernel, out_shape=(piece,) * 3, in_specs=[pl.BlockSp...  26.1 us

profile of v5, /device:TPU:0, one launch (start us, length us, event | category | flops | bytes accessed | tf_op | source)
XLA Modules:
  0.0 85.0 jit_solution(9295341145610449255)
XLA Ops:
  0.6 26.1 %build.1 = (bf16[1296,1152]{1,0:T(8,128)(2,1)S(1)}, bf16[1296,1152]{1,0:T(8,128)(2,1)S(1)}, bf16[1296,1152]{1,0:T(8,128)(2,1)S(1)}) custom-call(s32[16]{0:T(128)} %hub_hbm.1, s32[128,128]{1,0:T(8,128)} %bitcast.16, s32[128,128]{1,0:T(8,128)} %bitcast.17, f32[128,128]{1,0:T(8,128)} %bitcast.18), custom_call_target="tpu_custom_call" | custom-call | tf_op jit(solution)/shard_map/build/pallas_call | solution.py:142
  26.7 56.9 %step.1 = (f32[200,1024]{1,0:T(8,128)S(1)}, f32[200,512]{1,0:T(8,128)S(1)}, f32[107,512]{1,0:T(8,128)S(1)}, f32[1,512]{1,0:T(1,128)S(1)}, f32[1,107]{1,0:T(1,128)S(1)}) custom-call(bf16[1296,1152]{1,0:T(8,128)(2,1)S(1)} %get-tuple-element.18.hi_ref, bf16[1296,1152]{1,0:T(8,128)(2,1)S(1)} %get-tuple-element.19.mid_ref, ...), custom_call_target="tpu_custom_call" | custom-call | tf_op jit(solution)/shard_map/step/pallas_call | solution.py:444
  83.7 1.1 %emit.1 = (f32[200,1024]{1,0:T(8,128)}, f32[200,512]{1,0:T(8,128)}, f32[107,512]{1,0:T(8,128)}, f32[1,512]{1,0:T(1,128)}, f32[1,107]{1,0:T(1,128)}) custom-call(f32[200,1024]{1,0:T(8,128)S(1)} %get-tuple-element.21.refs_0_, f32[200,512]{1,0:T(8,128)S(1)} %get-tuple-element.22.refs_1_, f32[107,512]{1,0:T(8,128)S(1)} %get-tuple-element.23.refs_2_, ...), custom_call_target="tpu_custom_call" | custom-call | tf_op jit(solution)/shard_map/emit/pallas_call | solution.py:475

commit v6 on v5

--- a/solution.py
+++ b/solution.py
@@ -44,7 +44,7 @@
     return lax.dot_general(a, b, NT, preferred_element_type=F32)
 
 
-def build_kernel(hub_hbm, dst_hbm, src_hbm, w_hbm, hi_ref, mid_ref, lo_ref, hub_ref, dst_ref, src_ref, w_ref, row_ref, lane_ref, perm_ref, val_a, val_b, sem, *rest):
+def build_kernel(hub_hbm, dst_hbm, src_hbm, w_hbm, hi_ref, mid_ref, lo_ref, side_ref, hub_ref, dst_ref, src_ref, w_ref, row_ref, lane_ref, perm_ref, val_a, val_b, sem, *rest):
     row_smem, accs = rest[:8], rest[8:]
     loads = []
     for i, (a, b) in enumerate(((hub_hbm, hub_ref), (dst_hbm, dst_ref), (src_hbm, src_ref), (w_hbm, w_ref))):
@@ -128,22 +128,30 @@
             total = accs[0][part, :]
             for acc in accs[1:]:
                 total = total + acc[part, :]
-            for piece, ref in zip(split3(total), (hi_ref, mid_ref, lo_ref)):
-                ref[pl.ds(at, 48), t * 128:(t + 1) * 128] = piece
+            parts = split3(total)
+            if t < TILES - 1:
+                for piece, ref in zip(parts, (hi_ref, mid_ref, lo_ref)):
+                    ref[pl.ds(at, 48), t * 128:(t + 1) * 128] = piece
+            else:
+                side = parts[0].astype(F32)
+                for i, j in enumerate((1, 2, 0, 1, 0)):
+                    side = side + pltpu.roll(parts[j].astype(F32), (i + 1) * HUBS, 1)
+                side_ref[pl.ds(at, 48), :] = side.astype(BF16)
         return carry
 
     lax.fori_loop(0, TABLE // 48, finish, 0)
 
 
 def build(hub_ids, dst, src, w):
-    piece = jax.ShapeDtypeStruct((TABLE, COLS), BF16)
+    piece = jax.ShapeDtypeStruct((TABLE, NODES), BF16)
+    side = jax.ShapeDtypeStruct((TABLE, 128), BF16)
     square = lambda a: a.reshape(128, 128)
     table = pltpu.VMEM((128, 128), jnp.int32)
     return pl.pallas_call(
         build_kernel,
-        out_shape=(piece,) * 3,
+        out_shape=(piece, piece, piece, side),
         in_specs=[pl.BlockSpec(memory_space=pltpu.HBM)] * 4,
-        out_specs=(pl.BlockSpec(memory_space=pltpu.VMEM),) * 3,
+        out_specs=(pl.BlockSpec(memory_space=pltpu.VMEM),) * 4,
         scratch_shapes=[
             pltpu.SMEM((HUBS,), jnp.int32), table, table, pltpu.VMEM((128, 128), F32), table, table,
             pltpu.VMEM((8, 16, 128), jnp.int32), pltpu.VMEM((CHUNK * 8, 128), F32), pltpu.VMEM((CHUNK * 8, 128), F32),
@@ -155,10 +163,10 @@
 
 
 def step_kernel(
-    hi_ref, mid_ref, lo_ref, xt_hbm, w1_hbm, b1_hbm, w2t_hbm, dht_hbm, send_hbm, hub_hbm,
+    hi_ref, mid_ref, lo_ref, side_ref, xt_hbm, w1_hbm, b1_hbm, w2t_hbm, dht_hbm, send_hbm, hub_hbm,
     dxt_ref, dw1_ref, dw2t_ref, db1_ref, db2_ref,
     xt_ref, w1_ref, b1_ref, w2t_ref, dht_ref, send_ref, hub_ref,
-    row_s, pt_s, xs, xr, hs, hr, z_s, yt_s, d2_s, dhub_s, g2_s, g2h_s, rb, sb, ys, yr, dy_s, g1_s, sd, rd, dz1_s,
+    sent_s, pt_s, xs, xr, hs, hr, z_s, yt_s, d2_s, dhub_s, g2_s, g2h_s, rb, sb, ys, yr, dy_s, dyh_s, g1_s, sd, rd, dz1_s,
     a2, half2, got2, tot2, a1, half1, got1, tot1, load_sem, send_sem, recv_sem,
 ):
     me = lax.axis_index("graph")
@@ -195,22 +203,24 @@
             copy.wait()
 
     pieces = (hi_ref, mid_ref, lo_ref)
-    row_s[...] = jnp.full((1, 384), -1.0, F32)
-    row_s[:, :HALO] = send_ref[...].astype(F32)
     hub_local = hub_ref[...] - me * NODES
-    row_s[:, HALO:HALO + HUBS] = jnp.where((hub_local >= 0) & (hub_local < NODES), hub_local, -1).astype(F32)
-    row = row_s[...]
-    column = jnp.transpose(jnp.broadcast_to(row, (128, 384)))
-    lane = lax.broadcasted_iota(jnp.int32, (272, 128), 1).astype(F32)
+    hub_row = jnp.where((hub_local >= 0) & (hub_local < NODES), hub_local, -1).astype(F32)
+    hub_block = jnp.concatenate([hub_row, jnp.full((1, SEND - HUBS), -1.0, F32)], axis=1)
+    send_row = send_ref[...].astype(F32)
+    row = jnp.concatenate([jnp.where(me == q, hub_block, send_row[:, q * SEND:(q + 1) * SEND]) for q in range(4)], axis=1)
+    row3 = jnp.concatenate([hub_row] * 3 + [jnp.full((1, 128 - 3 * HUBS), -1.0, F32)], axis=1)
+    column = jnp.transpose(jnp.broadcast_to(jnp.concatenate([row, row3], axis=1), (128, 384)))
+    lane = lax.broadcasted_iota(jnp.int32, (HALO + 3 * HUBS, 128), 1).astype(F32)
     picks = jnp.concatenate(
-        [jnp.where(column[:272] == lane + float(j * 128), 1.0, 0.0).astype(BF16) for j in range(8)], axis=1)
+        [jnp.where(column[:HALO + 3 * HUBS] == lane + float(j * 128), 1.0, 0.0).astype(BF16) for j in range(8)], axis=1)
     xt = xt_ref[...]
-    sent = dot_nt(picks, xt).astype(BF16)
+    sent_s[...] = dot_nt(picks[:HALO], xt).astype(BF16).reshape(4, SEND, FIN)
     hub_col = column[HALO:HALO + HUBS]
     alias = [jnp.where((hub_col == row[:, j * 128:(j + 1) * 128]) & (hub_col >= 0.0), 1.0, 0.0) for j in range(2)]
+    own_hub_x = sent_s[me, :HUBS, :]
     for q in range(4):
-        xs[q, :SEND, :] = sent[q * SEND:(q + 1) * SEND]
-        xs[q, SEND:SEND + HUBS, :] = sent[HALO:]
+        xs[q, :SEND, :] = sent_s[q]
+        xs[q, SEND:SEND + HUBS, :] = own_hub_x
         part = alias[q // 2][:, (q % 2) * SEND:(q % 2 + 1) * SEND]
         xs[q, SEND + HUBS:, :SEND] = part.astype(BF16)
         xs[q, SEND + HUBS:, SEND:] = jnp.zeros((HUBS, FIN - SEND), BF16)
@@ -220,27 +230,26 @@
     for j, piece in enumerate(split3(dh)):
         d2_s[:, j * 128:(j + 1) * 128] = piece
     round_a = [remote(xs.at[q], xr.at[me], q) for q in peers]
-    hub_dh = dot(picks[HALO:], d2_s[...])
+    hub_dh = dot(picks[HALO:HALO + HUBS], d2_s[...])
     hs[...] = (hub_dh[:, :128] + hub_dh[:, 128:256]) + hub_dh[:, 256:]
     hr[me] = hs[...]
     db2 = jnp.sum(dh, axis=0, keepdims=True)
     round_a += [remote(hs, hr.at[me], q) for q in peers]
-    sub = lax.broadcasted_iota(jnp.int32, (NODES, 384), 0).astype(F32)
+    sub = lax.broadcasted_iota(jnp.int32, (NODES, HALO), 0).astype(F32)
     pt_s[...] = jnp.where(sub == row, 1.0, 0.0).astype(BF16)
 
-    def grad2(rows, cols, right):
-        a = dot(hi_ref[rows, cols], right[:, :256])
-        b = dot(mid_ref[rows, cols], right[:, :256])
-        c = dot(hi_ref[rows, cols], right[:, 256:]) + dot(lo_ref[rows, cols], right[:, :128])
+    def grad2(rows):
+        a = dot(hi_ref[rows, :], d2_s[:, :256])
+        b = dot(mid_ref[rows, :], d2_s[:, :256])
+        c = dot(hi_ref[rows, :], d2_s[:, 256:]) + dot(lo_ref[rows, :], d2_s[:, :128])
         return ((c + b[:, 128:]) + (a[:, 128:] + b[:, :128])) + a[:, :128]
 
-    own_cols, hub_cols = pl.ds(0, NODES), pl.ds(NODES, 128)
     far_rows = pl.ds(NODES, HALO + HUBS)
-    g2h_s[...] = grad2(far_rows, own_cols, d2_s)
+    g2h_s[...] = grad2(far_rows)
 
     def grad2_own(m, carry):
         at = pl.ds(pl.multiple_of(m * 256, 256), 256)
-        g2_s[at, :] = grad2(at, own_cols, d2_s)
+        g2_s[at, :] = grad2(at)
         return carry
 
     lax.fori_loop(0, 4, grad2_own, 0)
@@ -260,39 +269,44 @@
 
         lax.fori_loop(0, 4, turn, 0)
 
-    forward_own(hub_cols)
+    y_side = dot(z_s[:, :NODES], side_ref[:NODES, :])
     wait_all(round_a)
 
     halo_x = jnp.concatenate([xr[q, :SEND, :] for q in range(4)], axis=0)
-    hub_x = sent[HALO:].astype(F32)
+    hub_x = sent_s[me, :HUBS, :].astype(F32)
     for q in range(4):
         hub_x = hub_x + xr[q, SEND:SEND + HUBS, :].astype(F32)
     z_s[:, NODES:] = dot_nt(w1t, halo_x).astype(BF16)
-    z_hub = dot_nt(w1t, hub_x.astype(BF16)).astype(BF16)
+    z_hub = dot_nt(w1t, jnp.concatenate([hub_x.astype(BF16)] * 3, axis=0)).astype(BF16)
 
     def forward_far(at):
         z = z_s[:, NODES:]
         acc = yt_s[:, at]
         for ref in pieces:
             acc = acc + dot(z, ref[NODES:NODES + HALO, at])
-        for ref in pieces:
-            acc = acc + dot(z_hub, ref[NODES + HALO:, at])
-        yt_s[:, at] = acc
-
-    forward_far(hub_cols)
-    ys[...] = jnp.transpose(yt_s[:, NODES:])[:HUBS]
+        hub_rows = jnp.concatenate([ref[NODES + HALO:, at] for ref in pieces], axis=0)
+        yt_s[:, at] = acc + dot(z_hub, hub_rows)
+
+    y_side = y_side + dot(z_s[:, NODES:], side_ref[NODES:NODES + HALO, :])
+    y_side = jnp.transpose(y_side + dot(z_hub[:, :HUBS], side_ref[NODES + HALO:, :]))
+    ys[...] = (y_side[:HUBS] + y_side[HUBS:2 * HUBS]) + y_side[2 * HUBS:3 * HUBS]
     yr[me] = ys[...]
     hub_dh = (hr[0] + hr[1]) + (hr[2] + hr[3])
-    for j, piece in enumerate(split3(hub_dh)):
-        dhub_s[:HUBS, j * 128:(j + 1) * 128] = piece
-    dhub_s[HUBS:, :] = jnp.zeros((128 - HUBS, 384), BF16)
+    def side_by_side(x):
+        hi, mid, lo = split3(x)
+        return jnp.concatenate([hi, hi, hi, mid, mid, lo, jnp.zeros((32, x.shape[1]), BF16)], axis=0)
+
+    dhub_s[...] = side_by_side(hub_dh)
     round_b = [remote(ys, yr.at[me], q) for q in peers]
-    g2h_s[...] += grad2(far_rows, hub_cols, dhub_s)
+    g2h_s[...] += dot(side_ref[far_rows, :], dhub_s[...])
     far = g2h_s[:HALO, :]
     alias_row = jnp.concatenate([xr[q, SEND + HUBS:, :SEND] for q in range(4)], axis=1)
     hub_g2 = g2h_s[HALO:, :]
     for piece in split3(far):
         hub_g2 = hub_g2 + dot(alias_row, piece)
+    is_alias = dot(jnp.transpose(jnp.concatenate([alias_row.astype(F32), jnp.zeros((112, HALO), F32)], axis=0)).astype(BF16),
+                   jnp.ones((128, 128), BF16))
+    far = jnp.where(is_alias > 0.5, 0.0, far)
     for q in range(4):
         sb[q, :SEND, :] = far[q * SEND:(q + 1) * SEND]
         sb[q, SEND:, :] = hub_g2
@@ -304,40 +318,40 @@
 
     def grad2_hub(m, carry):
         at = pl.ds(pl.multiple_of(m * 256, 256), 256)
-        g2_s[at, :] += grad2(at, hub_cols, dhub_s)
+        g2_s[at, :] += dot(side_ref[at, :], dhub_s[...])
         return carry
 
     lax.fori_loop(0, 4, grad2_hub, 0)
     wait_all(round_b)
 
-    hub_dz2 = ((rb[0, SEND:, :] + rb[1, SEND:, :]) + (rb[2, SEND:, :] + rb[3, SEND:, :])).astype(BF16)
-    keep = lax.broadcasted_iota(jnp.int32, (4, SEND, 128), 0) != me
-    back = jnp.where(keep, rb[:, :SEND, :], 0.0).reshape(HALO, 128)
+    def returned(ref):
+        hub_sum = (ref[0, SEND:, :] + ref[1, SEND:, :]) + (ref[2, SEND:, :] + ref[3, SEND:, :])
+        ref[me, :HUBS, :] = hub_sum
+        ref[me, HUBS:SEND, :] = jnp.zeros((SEND - HUBS, hub_sum.shape[1]), F32)
+        return ref[:, :SEND, :].reshape(HALO, hub_sum.shape[1]), hub_sum
+
+    back, hub_sum = returned(rb)
+    hub_dz2 = hub_sum.astype(BF16)
     own = g2_s[...]
-    halo_pick = pt_s[:, :HALO]
-    hub_put = pt_s[:, HALO:HALO + HUBS]
     for piece in split3(back):
-        own = own + dot(halo_pick, piece)
-    is_hub = dot(hub_put, jnp.ones((HUBS, 128), BF16)) > 0.5
-    dz2 = jnp.where(is_hub, dot(hub_put, hub_dz2), own).astype(BF16)
+        own = own + dot(pt_s[...], piece)
+    dz2 = own.astype(BF16)
 
     y_hub = (yr[0] + yr[1]) + (yr[2] + yr[3])
     b1 = b1_ref[...]
     b1_col = jnp.transpose(jnp.broadcast_to(b1, (128, HID)))
-    for piece in split3(jnp.transpose(jnp.concatenate([y_hub, jnp.zeros((112, HID), F32)], axis=0))):
-        yt_s[:, :NODES] += dot(piece[:, :HUBS], picks[HALO:])
-    pre = yt_s[:, :NODES] + jnp.concatenate([b1_col] * 8, axis=1)
-    yt_s[:, :NODES] = pre
+    y_rows = jnp.concatenate([piece.astype(F32) for piece in split3(y_hub)] + [jnp.zeros((128 - 3 * HUBS, HID), F32)], axis=0)
+    y_own = dot(jnp.transpose(y_rows).astype(BF16)[:, :3 * HUBS], picks[HALO:])
+    pre = (yt_s[...] + y_own) + jnp.concatenate([b1_col] * 8, axis=1)
+    yt_s[...] = pre
     live = jnp.transpose(jnp.where(pre > 0.0, 1.0, 0.0))
     w2t = w2t_ref[...]
     dy = jnp.where(live > 0.5, dot(dz2[:, :OUT], w2t), 0.0)
     hub_dy = jnp.where(y_hub + b1 > 0.0, dot(hub_dz2[:, :OUT], w2t), 0.0)
     db1 = jnp.sum(dy, axis=0, keepdims=True)
     for j, piece in enumerate(split3(dy)):
-        dy_s[j, :NODES, :] = piece
-    for j, piece in enumerate(split3(hub_dy)):
-        dy_s[j, NODES:NODES + HUBS, :] = piece
-        dy_s[j, NODES + HUBS:, :] = jnp.zeros((112, HID), BF16)
+        dy_s[j] = piece
+    dyh_s[...] = side_by_side(hub_dy)
 
     class GroupSum:
         def __init__(self, own, half, got, total):
@@ -363,7 +377,8 @@
         acc = acc + dot(hi_ref[rows, :], dy_s[2, :, cols])
         acc = acc + dot(mid_ref[rows, :], dy_s[0, :, cols])
         acc = acc + dot(hi_ref[rows, :], dy_s[1, :, cols])
-        return acc + dot(hi_ref[rows, :], dy_s[0, :, cols])
+        acc = acc + dot(hi_ref[rows, :], dy_s[0, :, cols])
+        return acc + dot(side_ref[rows, :], dyh_s[:, cols])
 
     halves = (pl.ds(0, 256), pl.ds(256, 256))
     round_d = []
@@ -375,7 +390,7 @@
         rd[h, me] = sd[h, me]
         round_d.append([remote(sd.at[h, q], rd.at[h, me], q) for q in peers])
 
-    dw2t = jnp.transpose(dot(jnp.maximum(yt_s[:, :NODES], 0.0).astype(BF16), dz2))
+    dw2t = jnp.transpose(dot(jnp.maximum(yt_s[...], 0.0).astype(BF16), dz2))
     for h in range(2):
         a2[h, :112, :] = dw2t[:112, h * 256:(h + 1) * 256]
         a2[h, 112:, :128] = jnp.broadcast_to(db2, (8, 128))
@@ -388,14 +403,10 @@
     def finish(h):
         wait_all(round_d[h])
         cols = halves[h]
-        keep = lax.broadcasted_iota(jnp.int32, (4, SEND, 256), 0) != me
-        back = jnp.where(keep, rd[h, :, :SEND, :], 0.0).reshape(HALO, 256)
-        hub_back = (rd[h, 0, SEND:, :] + rd[h, 1, SEND:, :]) + (rd[h, 2, SEND:, :] + rd[h, 3, SEND:, :])
+        back, _ = returned(rd.at[h])
         dz1 = g1_s[:, cols]
         for piece in split3(back):
-            dz1 = dz1 + dot(halo_pick, piece)
-        for piece in split3(hub_back):
-            dz1 = dz1 + dot(hub_put, piece)
+            dz1 = dz1 + dot(pt_s[...], piece)
         dz1 = dz1.astype(BF16)
         dz1_s[:, cols] = dz1
         dw1 = dot(xt_ref[...], dz1)
@@ -436,7 +447,7 @@
     put(1)
 
 
-def step(hi, mid, lo, xt, w1, b1, w2t, dht, send, hubs):
+def step(hi, mid, lo, side, xt, w1, b1, w2t, dht, send, hubs):
     vmem = pl.BlockSpec(memory_space=pltpu.VMEM)
     out = lambda *shape: jax.ShapeDtypeStruct(shape, F32)
     f32 = lambda *shape: pltpu.VMEM(shape, F32)
@@ -444,22 +455,22 @@
     return pl.pallas_call(
         step_kernel,
         out_shape=(out(FIN, NODES), out(FIN, HID), out(OUT, HID), out(1, HID), out(1, OUT)),
-        in_specs=[vmem] * 3 + [pl.BlockSpec(memory_space=pltpu.HBM)] * 7,
+        in_specs=[vmem] * 4 + [pl.BlockSpec(memory_space=pltpu.HBM)] * 7,
         out_specs=(vmem,) * 5,
         scratch_shapes=[
             b16(FIN, NODES), b16(FIN, HID), f32(1, HID), b16(OUT, HID), f32(OUT, NODES),
             pltpu.VMEM((1, HALO), jnp.int32), pltpu.VMEM((1, HUBS), jnp.int32),
-            f32(1, 384), b16(NODES, 384), b16(4, 96, FIN), b16(4, 96, FIN), f32(HUBS, 128), f32(4, HUBS, 128),
-            b16(HID, NODES + HALO), f32(HID, COLS), b16(NODES, 384), b16(128, 384), f32(NODES, 128), f32(HALO + HUBS, 128),
+            b16(4, SEND, FIN), b16(NODES, HALO), b16(4, 96, FIN), b16(4, 96, FIN), f32(HUBS, 128), f32(4, HUBS, 128),
+            b16(HID, NODES + HALO), f32(HID, NODES), b16(NODES, 384), b16(128, 128), f32(NODES, 128), f32(HALO + HUBS, 128),
             f32(4, SEND + HUBS, 128), f32(4, SEND + HUBS, 128), f32(HUBS, HID), f32(4, HUBS, HID),
-            b16(3, COLS, HID), f32(NODES, HID), f32(2, 4, SEND + HUBS, 256), f32(2, 4, SEND + HUBS, 256), b16(NODES, HID),
+            b16(3, NODES, HID), b16(128, HID), f32(NODES, HID), f32(2, 4, SEND + HUBS, 256), f32(2, 4, SEND + HUBS, 256), b16(NODES, HID),
             f32(2, 120, 256), f32(120, 256), f32(2, 120, 256), f32(2, 120, 256),
             f32(2, 2, 208, 128), f32(2, 208, 128), f32(2, 2, 208, 128), f32(2, 2, 208, 128),
             pltpu.SemaphoreType.DMA((7,)), pltpu.SemaphoreType.DMA((28,)), pltpu.SemaphoreType.DMA((28,)),
         ],
         compiler_params=pltpu.CompilerParams(collective_id=0, has_side_effects=True, vmem_limit_bytes=STEP_VMEM),
         name="step",
-    )(hi, mid, lo, *(in_hbm(a) for a in (xt, w1, b1, w2t, dht, send, hubs)))
+    )(hi, mid, lo, side, *(in_hbm(a) for a in (xt, w1, b1, w2t, dht, send, hubs)))
 
 
 def emit_kernel(*refs):
@@ -491,9 +502,9 @@
     replicated = P()
 
     def device_step(x, dst, src, w, send, hub_ids, w_first, b_first, w_second, dy_out):
-        hi, mid, lo = build(hub_ids, dst, src, w)
+        table = build(hub_ids, dst, src, w)
         dx, dw1, dw2, db1, db2 = emit(*step(
-            hi, mid, lo, x.T, w_first, b_first.reshape(1, HID), w_second.T, dy_out.T, send.reshape(1, HALO), hub_ids.reshape(1, HUBS)))
+            *table, x.T, w_first, b_first.reshape(1, HID), w_second.T, dy_out.T, send.reshape(1, HALO), hub_ids.reshape(1, HUBS)))
         return dx.T, dw1, dw2.T, db1.reshape(HID), db2.reshape(OUT)
 
     return jax.shard_map(

time: 85.3 us -> 77.7 us (0.911)
  Pallas kernels: 84.2 us -> 75.9 us
    pallas_call x1, Pallas kernels: 56.9 us -> 45.6 us  [step(): pl.pallas_call(step_kernel, out_shape=(out(FIN, NODES), out(FIN, HID), ou...]
    pallas_call x1, Pallas kernels: 26.1 us -> 29.2 us  [build(): pl.pallas_call(build_kernel, out_shape=(piece, piece, piece, side), in_sp...]
where the time goes in v6:
time: 77.7 us; the launch traced here: 76.7 us
  Pallas kernels  75.9 us (98%)
  between operations  0.81 us (1%)
    pallas_call x1, Pallas kernels, step(): pl.pallas_call(step_kernel, out_shape=(out(FIN, NODES), out(FIN, HID), ou...  45.6 us
    pallas_call x1, Pallas kernels, build(): pl.pallas_call(build_kernel, out_shape=(piece, piece, piece, side), in_sp...  29.2 us

profile of v6, /device:TPU:0, one launch (start us, length us, event | category | flops | bytes accessed | tf_op | source)
XLA Modules:
  0.0 76.7 jit_solution(4425354892570512457)
XLA Ops:
  0.6 29.2 %build.1 = (bf16[1296,1024]{1,0:T(8,128)(2,1)S(1)}, bf16[1296,1024]{1,0:T(8,128)(2,1)S(1)}, bf16[1296,1024]{1,0:T(8,128)(2,1)S(1)}, bf16[1296,128]{1,0:T(8,128)(2,1)S(1)}) custom-call(s32[16]{0:T(128)} %hub_hbm.1, s32[128,128]{1,0:T(8,128)} %bitcast.16, s32[128,128]{1,0:T(8,128)} %bitcast.17, f32[128,128]{1,0:T(8,128)} %bitcast.18), custom_call_target="tpu_custom_call" | custom-call | tf_op jit(solution)/shard_map/build/pallas_call | solution.py:150
  29.9 45.6 %step.1 = (f32[200,1024]{1,0:T(8,128)S(1)}, f32[200,512]{1,0:T(8,128)S(1)}, f32[107,512]{1,0:T(8,128)S(1)}, f32[1,512]{1,0:T(1,128)S(1)}, f32[1,107]{1,0:T(1,128)S(1)}) custom-call(bf16[1296,1024]{1,0:T(8,128)(2,1)S(1)} %get-tuple-element.19.hi_ref, bf16[1296,1024]{1,0:T(8,128)(2,1)S(1)} %get-tuple-element.20.mid_ref, ...), custom_call_target="tpu_custom_call" | custom-call | tf_op jit(solution)/shard_map/step/pallas_call | solution.py:455
  75.4 1.1 %emit.1 = (f32[200,1024]{1,0:T(8,128)}, f32[200,512]{1,0:T(8,128)}, f32[107,512]{1,0:T(8,128)}, f32[1,512]{1,0:T(1,128)}, f32[1,107]{1,0:T(1,128)}) custom-call(f32[200,1024]{1,0:T(8,128)S(1)} %get-tuple-element.23.refs_0_, f32[200,512]{1,0:T(8,128)S(1)} %get-tuple-element.24.refs_1_, f32[107,512]{1,0:T(8,128)S(1)} %get-tuple-element.25.refs_2_, ...), custom_call_target="tpu_custom_call" | custom-call | tf_op jit(solution)/shard_map/emit/pallas_call | solution.py:486
